TPU v7x, 8 devices: a whole 2x2x1 slice. The times are simulated.
8 devices in a mesh: dp: 1 (over z), w: 8 (over y, x, core).
Axes of the slice: x: 2, y: 2, z: 1, core: 2. Of those that a mesh axis runs over, the one named last changes fastest.
Arguments:
- hidden: bfloat16 [1024, 2048], P(('dp', 'w'))
- positions: int32 [1024], P(('dp', 'w'))
- k_cache: bfloat16 [2, 1024, 1, 256, 256], P(None, ('dp', 'w'))
- v_cache: bfloat16 [2, 1024, 1, 256, 256], P(None, ('dp', 'w'))
- attn_norm: float32 [2, 2048], P(None, 'w')
- w_query: bfloat16 [2, 2048, 2048], P(None, 'w')
- w_key: bfloat16 [2, 2048, 256], P(None, 'w')
- w_value: bfloat16 [2, 2048, 256], P(None, 'w')
- w_out: bfloat16 [2, 2048, 2048], P(None, 'w')
- mlp_norm: float32 [2, 2048], P(None, 'w')
- w_gate: bfloat16 [2, 2048, 16384], P(None, 'w')
- w_up: bfloat16 [2, 2048, 16384], P(None, 'w')
- w_down: bfloat16 [2, 16384, 2048], P(None, 'w')
Outputs:
- output 1: bfloat16 [1024, 2048], P(('dp', 'w'))
- output 2: bfloat16 [2, 1024, 1, 256, 256], P(None, ('dp', 'w'))
- output 3: bfloat16 [2, 1024, 1, 256, 256], P(None, ('dp', 'w'))
All inputs are finite; a program needn't handle non-finite values.
Results may differ from a plain program's by a relative error of at most 0.0168836.
Values are sent between devices in bfloat16 or wider.
A program may use at most 1 GiB of HBM per device.

v0:
```python
import jax
import jax.numpy as jnp
from jax import lax
from jax.sharding import PartitionSpec as P

EPS = 1e-6
ROPE_BASE = 10000.0


def rms_norm(hidden, gain):
    hid_f32 = hidden.astype(jnp.float32)
    mean_sq = jnp.mean(hid_f32 * hid_f32, axis=-1, keepdims=True)
    return (hid_f32 * lax.rsqrt(mean_sq + EPS) * (1.0 + gain)).astype(jnp.bfloat16)


def rope_tables(positions, head_dim):
    half_dim = head_dim // 2
    inv_freq = ROPE_BASE ** (-2.0 * jnp.arange(half_dim, dtype=jnp.float32) / head_dim)
    angles = positions.astype(jnp.float32)[:, None] * inv_freq[None, :]
    return jnp.cos(angles), jnp.sin(angles)


def apply_rope(vectors, cos_tab, sin_tab):
    half_dim = vectors.shape[-1] // 2
    lead_half = vectors[..., :half_dim]
    tail_half = vectors[..., half_dim:]
    cos_b = cos_tab[:, None, :]
    sin_b = sin_tab[:, None, :]
    return jnp.concatenate([lead_half * cos_b - tail_half * sin_b, tail_half * cos_b + lead_half * sin_b], axis=-1)


def attention_core(q_proj, k_proj, v_proj, positions, cos_tab, sin_tab, k_layer, v_layer):
    batch_rows, kv_heads, cache_len, head_dim = k_layer.shape
    num_heads = q_proj.shape[-1] // head_dim
    q_rot = apply_rope(q_proj.reshape(batch_rows, num_heads, head_dim), cos_tab, sin_tab)
    q_rot = (q_rot * head_dim ** -0.5).astype(jnp.bfloat16).reshape(batch_rows, kv_heads, num_heads // kv_heads, head_dim)
    k_rot = apply_rope(k_proj.reshape(batch_rows, kv_heads, head_dim), cos_tab, sin_tab).astype(jnp.bfloat16)
    v_new = v_proj.reshape(batch_rows, kv_heads, head_dim).astype(jnp.bfloat16)
    cache_steps = jnp.arange(cache_len)
    write_mask = (cache_steps[None, :] == positions[:, None])[:, None, :, None]
    k_layer = jnp.where(write_mask, k_rot[:, :, None, :], k_layer)
    v_layer = jnp.where(write_mask, v_new[:, :, None, :], v_layer)
    scores = jnp.einsum("bkge,bkse->bkgs", q_rot, k_layer, preferred_element_type=jnp.float32)
    is_valid = cache_steps[None, None, None, :] <= positions[:, None, None, None]
    scores = jnp.where(is_valid, scores, -1e30)
    row_max = jnp.max(scores, axis=-1, keepdims=True)
    attn_prob = jnp.exp(scores - row_max)
    row_sum = jnp.sum(attn_prob, axis=-1, keepdims=True)
    attn_vals = jnp.einsum("bkgs,bkse->bkge", attn_prob.astype(jnp.bfloat16), v_layer, preferred_element_type=jnp.float32)
    attn_vals = (attn_vals / row_sum).astype(jnp.bfloat16).reshape(batch_rows, num_heads * head_dim)
    return attn_vals, k_layer, v_layer


def gather_rows(row_shard):
    return lax.all_gather(row_shard, "w", axis=0, tiled=True)


def solution(mesh):
    batch_spec = P(("dp", "w"))
    cache_spec = P(None, ("dp", "w"))
    gain_spec = P(None, "w")
    weight_spec = P(None, "w", None)

    def per_device(hidden, positions, k_cache, v_cache, attn_norm, w_query, w_key, w_value, w_out, mlp_norm, w_gate, w_up, w_down):
        cos_tab, sin_tab = rope_tables(positions, k_cache.shape[-1])
        k_layers = []
        v_layers = []
        for layer_idx in range(k_cache.shape[0]):
            normed = rms_norm(hidden, gather_rows(attn_norm[layer_idx]))
            q_proj = jnp.dot(normed, gather_rows(w_query[layer_idx]), preferred_element_type=jnp.float32)
            k_proj = jnp.dot(normed, gather_rows(w_key[layer_idx]), preferred_element_type=jnp.float32)
            v_proj = jnp.dot(normed, gather_rows(w_value[layer_idx]), preferred_element_type=jnp.float32)
            attn_vals, k_layer, v_layer = attention_core(q_proj, k_proj, v_proj, positions, cos_tab, sin_tab, k_cache[layer_idx], v_cache[layer_idx])
            hid_mid = (hidden.astype(jnp.float32) + jnp.dot(attn_vals, gather_rows(w_out[layer_idx]), preferred_element_type=jnp.float32)).astype(jnp.bfloat16)
            normed_mlp = rms_norm(hid_mid, gather_rows(mlp_norm[layer_idx]))
            gate_pre = jnp.dot(normed_mlp, gather_rows(w_gate[layer_idx]), preferred_element_type=jnp.float32)
            up_pre = jnp.dot(normed_mlp, gather_rows(w_up[layer_idx]), preferred_element_type=jnp.float32)
            mlp_hidden = (jax.nn.gelu(gate_pre, approximate=True) * up_pre).astype(jnp.bfloat16)
            hidden = (hid_mid.astype(jnp.float32) + jnp.dot(mlp_hidden, gather_rows(w_down[layer_idx]), preferred_element_type=jnp.float32)).astype(jnp.bfloat16)
            k_layers.append(k_layer)
            v_layers.append(v_layer)
        return hidden, jnp.stack(k_layers), jnp.stack(v_layers)

    in_specs = (batch_spec, batch_spec, cache_spec, cache_spec, gain_spec, weight_spec, weight_spec, weight_spec, weight_spec, gain_spec, weight_spec, weight_spec, weight_spec)
    out_specs = (batch_spec, cache_spec, cache_spec)
    return jax.shard_map(per_device, mesh=mesh, in_specs=in_specs, out_specs=out_specs, check_vma=False)
```

profile of v0, /device:TPU:0, one launch (start us, length us, event | category | flops | bytes accessed | tf_op | source)
XLA Modules:
  0.0 2138.4 jit_solution(11778054475409973215)
XLA Ops:
  7.2 1.7 fusion.188
  9.0 1.7 fusion.189
  10.7 3.1 fusion.187
  13.9 3.2 fusion.186
  17.2 11.6 fusion.184
  28.8 12.0 fusion.185
  40.8 11.6 fusion.183
  52.5 0.7 all-gather.47.cloned.1.call-update
  53.3 0.7 all-gather.49.cloned.1.call-update
  54.6 0.7 all-gather.53.cloned.1.call-update
  55.9 0.7 all-gather.59.cloned.1.call-update
  57.2 13.7 all-gather
  71.0 10.9 all-gather.5
  81.8 10.9 all-gather.9
  92.7 10.7 all-gather.14
  104.7 1.6 convolution_bitcast_fusion.1
  106.7 1.6 convolution_convert_fusion.1
  108.3 4.8 fusion.62
  113.7 10.4 fusion.192
  124.2 1.1 slice-done.6
  125.3 1.2 slice-done.7
  126.5 16.5 fusion.28
  143.8 6.7 all-gather.39.cloned.1.call-done
  150.4 4.8 multiply_reduce_fusion.2
  155.2 294.7 %all-gather.41.cloned.1.call-done = bf16[1,2048,16384]{2,1,0:T(8,128)(2,1)} async-done(((bf16[1,256,16384]{2,1,0:T(8,128)(2,1)}), bf16[1,2048,16384]{2,1,0:T(8,128)(2,1)}) %all-gather.41.cloned.1.call-update) | async-done | bytes 67108880 | tf_op jit(solution)/shard_map/all_gather | solution.py:55
  449.9 27.9 %fusion.44 = f32[128,16384]{1,0:T(8,128)} fusion(bf16[1,2048,16384]{2,1,0:T(8,128)(2,1)} %all-gather.41.cloned.1.call-done, f32[128,2048]{1,0:T(8,128)S(1)} %get-tuple-element.42, f32[2048]{0:T(1024)S(1)} %bitcast.179, f32[128]{0:T(128)S(1)} %add_rsqrt_fusion.2), kind=kOutput, calls=%fused_computation.48 | convolution fusion | flops 8607498240 | bytes 76554752 | tf_op jit(solution)/shard_map/dot_general | solution.py:76
  477.8 271.6 %all-gather.45.cloned.1.call-done = bf16[1,16384,2048]{2,1,0:T(8,128)(2,1)} async-done(((bf16[1,2048,2048]{2,1,0:T(8,128)(2,1)}), bf16[1,16384,2048]{2,1,0:T(8,128)(2,1)}) %all-gather.45.cloned.1.call-update) | async-done | bytes 67108880 | tf_op jit(solution)/shard_map/all_gather | solution.py:55
  749.4 299.0 %all-gather.43.cloned.1.call-done = bf16[1,2048,16384]{2,1,0:T(8,128)(2,1)} async-done(((bf16[1,256,16384]{2,1,0:T(8,128)(2,1)}), bf16[1,2048,16384]{2,1,0:T(8,128)(2,1)}) %all-gather.43.cloned.1.call-update) | async-done | bytes 67108880 | tf_op jit(solution)/shard_map/all_gather | solution.py:55
  1048.4 46.0 %multiply_reduce_fusion.1 = (f32[128]{0:T(128)S(1)}, f32[128,2048]{1,0:T(8,128)S(1)}) fusion(f32[128,2048]{1,0:T(8,128)S(1)} %get-tuple-element.42, bf16[1,16384,2048]{2,1,0:T(8,128)(2,1)} %all-gather.45.cloned.1.call-done, f32[128,16384]{1,0:T(8,128)} %fusion.44, bf16[1,2048,16384]{2,1,0:T(8,128)(2,1)} %all-gather.43.cloned.1.call-done, ...), kind=kOutput, calls=%fused_computation.106 | convolution fusion | flops 17186160640 | bytes 144712704 | tf_op jit(solution)/shard_map/dot_general | solution.py:79
  1094.6 4.0 all-gather.47.cloned.1.call-done
  1098.6 4.6 fusion.58
  1103.6 14.4 all-gather.49.cloned.1.call-done
  1118.0 1.5 convolution_bitcast_fusion
  1119.9 17.9 all-gather.51.cloned.1.call-done
  1137.8 1.5 convolution_convert_fusion
  1139.5 10.2 fusion.195
  1149.6 8.8 fusion.26
  1159.2 28.8 %all-gather.53.cloned.1.call-done = bf16[1,2048,2048]{2,1,0:T(8,128)(2,1)} async-done(((bf16[1,256,2048]{2,1,0:T(8,128)(2,1)}), bf16[1,2048,2048]{2,1,0:T(8,128)(2,1)}) %all-gather.53.cloned.1.call-update) | async-done | bytes 8388624 | tf_op jit(solution)/shard_map/all_gather | solution.py:55
  1188.0 4.8 multiply_reduce_fusion
  1192.8 33.0 %broadcast_select_fusion.1 = (bf16[1,128,1,256,256]{4,3,1,2,0:T(8,128)(2,1)}, bf16[1,128,1,256,256]{4,3,1,2,0:T(8,128)(2,1)}, bf16[1,128,1,256,256]{4,3,2,1,0:T(8,128)(2,1)}) fusion(pred[128,256]{1,0:T(8,128)(4,1)S(1)} %get-tuple-element.38, bf16[2,128,1,256,256]{4,3,1,2,0:T(8,128)(2,1)} %bitcast.168, bf16[128,256]{1,0:T(8,128)(2,1)S(1)} %pad_maximum_fusion.1, ...), kind=kLoop, calls=%fused_computation.31 | loop fusion | flops 25165824 | bytes 100892672 | tf_op jit(solution)/shard_map/jit(_where)/select_n | solution.py:41
  1225.8 23.0 %maximum_bitcast_fusion = bf16[2,128,1,256,256]{4,3,2,1,0:T(8,128)(2,1)} fusion(bf16[1,128,1,256,256]{4,3,1,2,0:T(8,128)(2,1)} %get-tuple-element.7, bf16[1,128,1,256,256]{4,3,1,2,0:T(8,128)(2,1)} %get-tuple-element.6), kind=kLoop, calls=%fused_computation.14 | loop fusion | flops 16777216 | bytes 67108864
  1248.8 11.9 bitcast_select_fusion
  1260.7 23.0 %pad_maximum_fusion = bf16[2,128,1,256,256]{4,3,2,1,0:T(8,128)(2,1)} fusion(bf16[1,128,1,256,256]{4,3,2,1,0:T(8,128)(2,1)} %bitcast_select_fusion, bf16[1,128,1,256,256]{4,3,2,1,0:T(8,128)(2,1)} %get-tuple-element.30), kind=kLoop, calls=%fused_computation.15 | loop fusion | flops 16777216 | bytes 67108864 | tf_op jit(solution)/shard_map/stack | solution.py:82
  1283.6 203.3 %all-gather.55.cloned.1.call-done = bf16[1,2048,16384]{2,1,0:T(8,128)(2,1)} async-done(((bf16[1,256,16384]{2,1,0:T(8,128)(2,1)}), bf16[1,2048,16384]{2,1,0:T(8,128)(2,1)}) %all-gather.55.cloned.1.call-update) | async-done | bytes 67108880 | tf_op jit(solution)/shard_map/all_gather | solution.py:55
  1487.0 27.9 %fusion.53 = f32[128,16384]{1,0:T(8,128)} fusion(bf16[1,2048,16384]{2,1,0:T(8,128)(2,1)} %all-gather.55.cloned.1.call-done, f32[128,2048]{1,0:T(8,128)S(1)} %get-tuple-element.48, f32[2048]{0:T(1024)S(1)} %bitcast.177, f32[128]{0:T(128)S(1)} %add_rsqrt_fusion), kind=kOutput, calls=%fused_computation.55 | convolution fusion | flops 8607498240 | bytes 76554752 | tf_op jit(solution)/shard_map/dot_general | solution.py:76
  1514.8 271.2 %all-gather.59.cloned.1.call-done = bf16[1,16384,2048]{2,1,0:T(8,128)(2,1)} async-done(((bf16[1,2048,2048]{2,1,0:T(8,128)(2,1)}), bf16[1,16384,2048]{2,1,0:T(8,128)(2,1)}) %all-gather.59.cloned.1.call-update) | async-done | bytes 67108880 | tf_op jit(solution)/shard_map/all_gather | solution.py:55
  1786.0 298.9 %all-gather.57.cloned.1.call-done = bf16[1,2048,16384]{2,1,0:T(8,128)(2,1)} async-done(((bf16[1,256,16384]{2,1,0:T(8,128)(2,1)}), bf16[1,2048,16384]{2,1,0:T(8,128)(2,1)}) %all-gather.57.cloned.1.call-update) | async-done | bytes 67108880 | tf_op jit(solution)/shard_map/all_gather | solution.py:55
  2084.9 46.9 %fusion.100 = bf16[128,2048]{1,0:T(8,128)(2,1)} fusion(f32[128,2048]{1,0:T(8,128)S(1)} %get-tuple-element.48, bf16[1,16384,2048]{2,1,0:T(8,128)(2,1)} %all-gather.59.cloned.1.call-done, f32[128,16384]{1,0:T(8,128)} %fusion.53, bf16[1,2048,16384]{2,1,0:T(8,128)(2,1)} %all-gather.57.cloned.1.call-done, f32[2048]{0:T(1024)S(1)} %bitcast.178, ...), kind=kOutput, calls=%fused_computation.76 | convolution fusion | flops 17185374208 | bytes 144187904 | tf_op jit(solution)/shard_map/dot_general | solution.py:79
  (84 shorter events, 6.8 us)
Async XLA Ops:
  7.2 97.6 %all-gather.35.cloned.1.call-start = ((), (), s32[]{:S(2)}) async-start(), calls=%async_computation.1 | async-start | bytes 1179648 | tf_op jit(solution)/shard_map/all_gather | solution.py:55
  8.9 97.8 %all-gather.37.cloned.1.call-start = ((), (), s32[]{:S(2)}) async-start(), calls=%async_computation.2 | async-start | bytes 1179648 | tf_op jit(solution)/shard_map/all_gather | solution.py:55
  10.7 97.6 %all-gather.33.cloned.1.call-start = ((), (), s32[]{:S(2)}) async-start(), calls=%async_computation | async-start | bytes 9437184 | tf_op jit(solution)/shard_map/all_gather | solution.py:55
  13.9 136.5 %all-gather.39.cloned.1.call-start = ((), (), s32[]{:S(2)}) async-start(), calls=%async_computation.3 | async-start | bytes 9437184 | tf_op jit(solution)/shard_map/all_gather | solution.py:55
  17.1 432.8 %all-gather.41.cloned.1.call-start = ((), (), s32[]{:S(2)}) async-start(), calls=%async_computation.4 | async-start | bytes 75497472 | tf_op jit(solution)/shard_map/all_gather | solution.py:55
  28.8 720.6 %all-gather.45.cloned.1.call-start = ((), (), s32[]{:S(2)}) async-start(), calls=%async_computation.6 | async-start | bytes 75497472 | tf_op jit(solution)/shard_map/all_gather | solution.py:55
  40.8 1007.6 %all-gather.43.cloned.1.call-start = ((), (), s32[]{:S(2)}) async-start(), calls=%async_computation.5 | async-start | bytes 75497472 | tf_op jit(solution)/shard_map/all_gather | solution.py:55
  52.4 4.8 copy-start.6
  52.4 4.8 copy-start.4
  52.4 18.5 copy-start.5
  52.5 51.0 %copy-start = (bf16[128,2048]{1,0:T(8,128)(2,1)S(1)}, bf16[128,2048]{1,0:T(8,128)(2,1)}, u32[]{:S(2)}) copy-start(bf16[128,2048]{1,0:T(8,128)(2,1)} %param.13) | copy-start | bytes 1572868
  52.5 1046.1 %all-gather.47.cloned.1.call-start = ((), (), s32[]{:S(2)}) async-start(), calls=%async_computation.7 | async-start | bytes 9437184 | tf_op jit(solution)/shard_map/all_gather | solution.py:55
  53.2 1064.8 %all-gather.49.cloned.1.call-start = ((), (), s32[]{:S(2)}) async-start(), calls=%async_computation.8 | async-start | bytes 1179648 | tf_op jit(solution)/shard_map/all_gather | solution.py:55
  54.0 1083.8 %all-gather.51.cloned.1.call-start = ((), (), s32[]{:S(2)}) async-start(), calls=%async_computation.9 | async-start | bytes 1179648 | tf_op jit(solution)/shard_map/all_gather | solution.py:55
  54.6 1133.4 %all-gather.53.cloned.1.call-start = ((), (), s32[]{:S(2)}) async-start(), calls=%async_computation.10 | async-start | bytes 9437184 | tf_op jit(solution)/shard_map/all_gather | solution.py:55
  55.3 1431.7 %all-gather.55.cloned.1.call-start = ((), (), s32[]{:S(2)}) async-start(), calls=%async_computation.11 | async-start | bytes 75497472 | tf_op jit(solution)/shard_map/all_gather | solution.py:55
  55.9 1730.1 %all-gather.59.cloned.1.call-start = ((), (), s32[]{:S(2)}) async-start(), calls=%async_computation.13 | async-start | bytes 75497472 | tf_op jit(solution)/shard_map/all_gather | solution.py:55
  56.6 2028.3 %all-gather.57.cloned.1.call-start = ((), (), s32[]{:S(2)}) async-start(), calls=%async_computation.12 | async-start | bytes 75497472 | tf_op jit(solution)/shard_map/all_gather | solution.py:55
  108.3 15.9 copy-start.2
  108.3 15.9 slice-start
  108.3 15.9 slice-start.1
  113.2 11.0 slice-start.2
  113.7 10.5 slice-start.3
  113.7 10.5 slice-start.4
  113.7 10.5 slice-start.5
  113.7 11.6 slice-start.6
  113.7 12.8 slice-start.7
  1158.4 34.4 %copy-start.3 = (bf16[128,256]{1,0:T(8,128)(2,1)S(1)}, bf16[128,256]{1,0:T(8,128)(2,1)}, u32[]{:S(2)}) copy-start(bf16[128,256]{1,0:T(8,128)(2,1)} %copy-done.2) | copy-start | bytes 196612
  1260.7 226.3 %copy-start.1 = (f32[1,2048]{1,0:T(1,128)S(1)}, f32[1,2048]{1,0:T(1,128)}, u32[]{:S(2)}) copy-start(f32[1,2048]{1,0:T(1,128)} %broadcast_add_fusion) | copy-start | bytes 24580
Sparse Core Ops, SparseCore 0:
  9.8 20.3 all-gather.34
  32.0 17.5 all-gather.36
  51.4 48.8 all-gather.32
  102.0 48.3 all-gather.38
  152.6 297.2 all-gather.40
  452.1 297.1 all-gather.44
  751.2 297.1 all-gather.42
  1050.2 48.3 all-gather.46
  1100.4 17.5 all-gather.48
  1120.2 17.5 all-gather.50
  1139.6 48.3 all-gather.52
  1189.7 297.2 all-gather.54
  1488.8 297.1 all-gather.58
  1787.7 297.1 all-gather.56
where the time goes:
time: 2140 us
  waiting for transfers between devices  1720 us (80%)
  matrix products  220 us (10%)
  other arithmetic  94.4 us (4%)
  local copies, waits for them, and re-layouts  48.1 us (2%)
  blocking collectives  46.2 us (2%)
    all_gather x14, waiting for transfers between devices, gather_rows(): return lax.all_gather(row_shard, 'w', axis=0, tiled=True)  1710 us
    dot_general x2, matrix products, per_device(): jnp.dot(mlp_hidden, gather_rows(w_down[layer_idx]), preferred_element_typ...  92.9 us
    dot_general x2, matrix products, per_device(): jnp.dot(normed_mlp, gather_rows(w_gate[layer_idx]), preferred_element_typ...  55.7 us
    all_gather x4, blocking collectives, gather_rows(): return lax.all_gather(row_shard, 'w', axis=0, tiled=True)  46.2 us
  transfers between devices with their start and end apart: 14, of which 11 were waited for; matrix products, arithmetic and copies ran while one was open for 15% of the time, Pallas kernels for 0%

commit v1 on v0

--- a/solution.py
+++ b/solution.py
@@ -55,28 +55,47 @@
     return lax.all_gather(row_shard, "w", axis=0, tiled=True)
 
 
+def exchange_columns(weight_shard, rank, ways):
+    rows, cols = weight_shard.shape
+    width = cols // ways
+    whole = jnp.zeros((rows * ways, width), weight_shard.dtype)
+    for mask in range(ways):
+        peer = jnp.bitwise_xor(rank, mask)
+        block = lax.dynamic_slice(weight_shard, (0, peer * width), (rows, width))
+        if mask:
+            block = lax.ppermute(block, "w", [(s, s ^ mask) for s in range(ways)])
+        whole = lax.dynamic_update_slice(whole, block, (peer * rows, 0))
+    return whole
+
+
 def solution(mesh):
     batch_spec = P(("dp", "w"))
     cache_spec = P(None, ("dp", "w"))
     gain_spec = P(None, "w")
     weight_spec = P(None, "w", None)
+    ways = mesh.shape["w"]
 
     def per_device(hidden, positions, k_cache, v_cache, attn_norm, w_query, w_key, w_value, w_out, mlp_norm, w_gate, w_up, w_down):
+        rank = lax.axis_index("w")
         cos_tab, sin_tab = rope_tables(positions, k_cache.shape[-1])
         k_layers = []
         v_layers = []
         for layer_idx in range(k_cache.shape[0]):
+            gate_cols = exchange_columns(w_gate[layer_idx], rank, ways)
+            up_cols = exchange_columns(w_up[layer_idx], rank, ways)
             normed = rms_norm(hidden, gather_rows(attn_norm[layer_idx]))
             q_proj = jnp.dot(normed, gather_rows(w_query[layer_idx]), preferred_element_type=jnp.float32)
             k_proj = jnp.dot(normed, gather_rows(w_key[layer_idx]), preferred_element_type=jnp.float32)
             v_proj = jnp.dot(normed, gather_rows(w_value[layer_idx]), preferred_element_type=jnp.float32)
             attn_vals, k_layer, v_layer = attention_core(q_proj, k_proj, v_proj, positions, cos_tab, sin_tab, k_cache[layer_idx], v_cache[layer_idx])
             hid_mid = (hidden.astype(jnp.float32) + jnp.dot(attn_vals, gather_rows(w_out[layer_idx]), preferred_element_type=jnp.float32)).astype(jnp.bfloat16)
-            normed_mlp = rms_norm(hid_mid, gather_rows(mlp_norm[layer_idx]))
-            gate_pre = jnp.dot(normed_mlp, gather_rows(w_gate[layer_idx]), preferred_element_type=jnp.float32)
-            up_pre = jnp.dot(normed_mlp, gather_rows(w_up[layer_idx]), preferred_element_type=jnp.float32)
+            normed_mlp = gather_rows(rms_norm(hid_mid, gather_rows(mlp_norm[layer_idx])))
+            gate_pre = jnp.dot(normed_mlp, gate_cols, preferred_element_type=jnp.float32)
+            up_pre = jnp.dot(normed_mlp, up_cols, preferred_element_type=jnp.float32)
             mlp_hidden = (jax.nn.gelu(gate_pre, approximate=True) * up_pre).astype(jnp.bfloat16)
-            hidden = (hid_mid.astype(jnp.float32) + jnp.dot(mlp_hidden, gather_rows(w_down[layer_idx]), preferred_element_type=jnp.float32)).astype(jnp.bfloat16)
+            partial = jnp.dot(mlp_hidden, w_down[layer_idx], preferred_element_type=jnp.float32)
+            mlp_out = lax.psum_scatter(partial, "w", scatter_dimension=0, tiled=True)
+            hidden = (hid_mid.astype(jnp.float32) + mlp_out).astype(jnp.bfloat16)
             k_layers.append(k_layer)
             v_layers.append(v_layer)
         return hidden, jnp.stack(k_layers), jnp.stack(v_layers)

time: 2140 us -> 1010 us (0.47)
  waiting for transfers between devices: 1720 us -> 539 us
  local copies, waits for them, and re-layouts: 48.1 us -> 116 us
  matrix products: 220 us -> 162 us
  starting transfers between devices: 0.56 us -> 26.9 us
    all_gather x14 -> x10, waiting for transfers between devices: 1710 us -> 164 us  [gather_rows(): return lax.all_gather(row_shard, 'w', axis=0, tiled=True)]
    ppermute x0 -> x28, waiting for transfers between devices: none -> 334 us  [exchange_columns(): block = lax.ppermute(block, 'w', [(s, s ^ mask) for s in range(ways)])]
    dot_general x4, matrix products: 149 us -> 91.7 us  [the longest x2 62.3 us: per_device(): jnp.dot(mlp_hidden, w_down[layer_idx], preferred_element_type=jnp.float32)]
    dynamic_update_slice x0 -> x32, local copies, waits for them, and re-layouts: none -> 45.3 us  [exchange_columns(): whole = lax.dynamic_update_slice(whole, block, (peer * rows, 0))]
    reduce_scatter x0 -> x2, waiting for transfers between devices: none -> 37.7 us  [per_device(): mlp_out = lax.psum_scatter(partial, 'w', scatter_dimension=0, tiled=True)]
    ppermute x0 -> x28, starting transfers between devices: none -> 25.9 us  [exchange_columns(): block = lax.ppermute(block, 'w', [(s, s ^ mask) for s in range(ways)])]
  transfers between devices with their start and end apart: 14 -> 40, of which waited for: 11 -> 18; matrix products, arithmetic and copies ran while one was open for 15% -> 26% of each run, Pallas kernels for 0% -> 0%
where the time goes in v1:
time: 1010 us; the launch traced here: 1000 us
  waiting for transfers between devices  539 us (53%)
  matrix products  162 us (16%)
  local copies, waits for them, and re-layouts  116 us (11%)
  other arithmetic  98.9 us (10%)
  blocking collectives  45.4 us (4%)
  starting transfers between devices  26.9 us (3%)
  between operations  14.9 us (1%)
    ppermute x28, waiting for transfers between devices, exchange_columns(): block = lax.ppermute(block, 'w', [(s, s ^ mask) for s in range(ways)])  334 us
    all_gather x10, waiting for transfers between devices, gather_rows(): return lax.all_gather(row_shard, 'w', axis=0, tiled=True)  164 us
    dot_general x2, matrix products, per_device(): jnp.dot(mlp_hidden, w_down[layer_idx], preferred_element_type=jnp.float32)  62.3 us
    all_gather x4, blocking collectives, gather_rows(): return lax.all_gather(row_shard, 'w', axis=0, tiled=True)  45.4 us
    dynamic_update_slice x32, local copies, waits for them, and re-layouts, exchange_columns(): whole = lax.dynamic_update_slice(whole, block, (peer * rows, 0))  45.3 us
    reduce_scatter x2, waiting for transfers between devices, per_device(): mlp_out = lax.psum_scatter(partial, 'w', scatter_dimension=0, tiled=True)  37.7 us
    select_n x1, other arithmetic, attention_core(): k_layer = jnp.where(write_mask, k_rot[:, :, None, :], k_layer)  33 us
    dot_general x2, matrix products, per_device(): jnp.dot(normed_mlp, gate_cols, preferred_element_type=jnp.float32)  29.5 us
  transfers between devices with their start and end apart: 40, of which 18 were waited for; matrix products, arithmetic and copies ran while one was open for 26% of the time, Pallas kernels for 0%

profile of v1, /device:TPU:0, one launch (start us, length us, event | category | flops | bytes accessed | tf_op | source)
XLA Modules:
  0.0 1003.6 jit_solution(18097909551673230290)
XLA Ops:
  17.2 9.3 fusion.148
  26.5 3.3 copy-done
  33.4 12.8 %all-gather.5 = f32[1,2048]{1,0:T(1,128)S(1)} all-gather(f32[1,256]{1,0:T(1,128)S(1)} %get-tuple-element.60), channel_id=7, replica_groups=mesh['dp'=1,'w'=8] {'w'}, dimensions={1}, use_global_device_ids=true | all-gather | bytes 9216 | tf_op jit(solution)/shard_map/all_gather | solution.py:55
  46.2 10.7 %all-gather = f32[1,2048]{1,0:T(1,128)S(1)} all-gather(f32[1,256]{1,0:T(1,128)S(1)} %get-tuple-element.62), channel_id=2, replica_groups=mesh['dp'=1,'w'=8] {'w'}, dimensions={1}, use_global_device_ids=true | all-gather | bytes 9216 | tf_op jit(solution)/shard_map/all_gather | solution.py:55
  61.2 39.8 %all-gather.27.cloned.1.call-done = bf16[1,2048,2048]{2,1,0:T(8,128)(2,1)} async-done(((bf16[1,256,2048]{2,1,0:T(8,128)(2,1)}), bf16[1,2048,2048]{2,1,0:T(8,128)(2,1)}) %all-gather.27.cloned.1.call-update) | async-done | bytes 8388624 | tf_op jit(solution)/shard_map/all_gather | solution.py:55
  101.0 4.8 fusion.42
  106.4 10.2 %fusion.156 = (f32[128,8]{1,0:T(8,128)S(1)}, f32[128,8,256]{2,1,0:T(8,128)S(1)}) fusion(pred[128,256]{1,0:T(8,128)(4,1)S(1)} %get-tuple-element.66, bf16[2,128,1,256,256]{4,3,1,2,0:T(8,128)(2,1)} %bitcast.193, bf16[128,256]{1,0:T(8,128)(2,1)S(1)} %pad_maximum_fusion.1, f32[128,8,128]{2,1,0:T(8,128)S(1)} %get-tuple-element.49, ...), kind=kOutput, calls=%fused_computation.243 | convolution fusion | flops 143916032 | bytes 19009536 | tf_op jit(solution)/shard_map/bkge,bkse->bkgs/dot_general | solution.py:43
  119.2 16.5 %fusion.4 = f32[128,8,256]{2,1,0:T(8,128)S(1)} fusion(pred[128,256]{1,0:T(8,128)(4,1)S(1)} %get-tuple-element.66, bf16[2,128,1,256,256]{4,3,1,2,0:T(8,128)(2,1)S(1)} %bitcast.192, bf16[128,256]{1,0:T(8,128)(2,1)S(1)} %convolution_convert_fusion.1, f32[128,8,256]{2,1,0:T(8,128)S(1)} %get-tuple-element.68, f32[128,8]{1,0:T(8,128)S(1)} %get-tuple-element.67), kind=kOutput, calls=%fused_computation.10 | convolution fusion | flops 143130624 | bytes 19038208 | tf_op jit(solution)/shard_map/bkgs,bkse->bkge/dot_general | solution.py:49
  136.4 14.8 %all-gather.33.cloned.1.call-done = bf16[1,2048,2048]{2,1,0:T(8,128)(2,1)} async-done(((bf16[1,256,2048]{2,1,0:T(8,128)(2,1)}), bf16[1,2048,2048]{2,1,0:T(8,128)(2,1)}) %all-gather.33.cloned.1.call-update) | async-done | bytes 8388624 | tf_op jit(solution)/shard_map/all_gather | solution.py:55
  151.2 4.8 multiply_reduce_fusion.1
  157.5 9.3 fusion.149
  166.8 3.2 copy-done.1
  176.3 4.5 broadcast.240.clone
  183.1 4.4 broadcast.240.clone.1
  196.1 12.9 %collective-permute-done.1 = bf16[256,2048]{1,0:T(8,128)(2,1)} collective-permute-done((bf16[256,2048]{1,0:T(8,128)(2,1)}, bf16[256,2048]{1,0:T(8,128)(2,1)}, u32[]{:S(2)}, u32[]{:S(2)}) %collective-permute-start.1) | collective-permute-done | bytes 1048608 | tf_op jit(solution)/shard_map/ppermute | solution.py:66
  212.7 41.2 %collective-permute-done.8 = bf16[256,2048]{1,0:T(8,128)(2,1)} collective-permute-done((bf16[256,2048]{1,0:T(8,128)(2,1)}, bf16[256,2048]{1,0:T(8,128)(2,1)}, u32[]{:S(2)}, u32[]{:S(2)}) %collective-permute-start.8) | collective-permute-done | bytes 1048608 | tf_op jit(solution)/shard_map/ppermute | solution.py:66
  260.3 15.6 %collective-permute-done.9 = bf16[256,2048]{1,0:T(8,128)(2,1)S(1)} collective-permute-done((bf16[256,2048]{1,0:T(8,128)(2,1)}, bf16[256,2048]{1,0:T(8,128)(2,1)S(1)}, u32[]{:S(2)}, u32[]{:S(2)}) %collective-permute-start.9) | collective-permute-done | bytes 1048608 | tf_op jit(solution)/shard_map/ppermute | solution.py:66
  285.7 105.8 %collective-permute-done.11 = bf16[256,2048]{1,0:T(8,128)(2,1)S(1)} collective-permute-done((bf16[256,2048]{1,0:T(8,128)(2,1)S(1)}, bf16[256,2048]{1,0:T(8,128)(2,1)S(1)}, u32[]{:S(2)}, u32[]{:S(2)}) %collective-permute-start.11) | collective-permute-done | bytes 1048608 | tf_op jit(solution)/shard_map/ppermute | solution.py:66
  396.8 14.8 %fusion.158 = f32[1024,2048]{1,0:T(8,128)} fusion(bf16[1024,2048]{1,0:T(8,128)(2,1)} %all-gather.23.cloned.1.call-done, bf16[2048,2048]{1,0:T(8,128)(2,1)} %constant_dynamic-update-slice_fusion.21), kind=kOutput, calls=%fused_computation.245 | convolution fusion | flops 8589934592 | bytes 20971520 | tf_op jit(solution)/shard_map/dot_general | solution.py:93
  411.6 31.1 %fusion.38 = f32[1024,2048]{1,0:T(8,128)} fusion(bf16[2,2048,2048]{2,1,0:T(8,128)(2,1)} %param.25, f32[1024,2048]{1,0:T(8,128)} %fusion.158, bf16[1024,2048]{1,0:T(8,128)(2,1)} %all-gather.23.cloned.1.call-done, bf16[2048,2048]{1,0:T(8,128)(2,1)} %constant_dynamic-update-slice_fusion.13), kind=kOutput, calls=%fused_computation.50 | convolution fusion | flops 17200840704 | bytes 37748736 | tf_op jit(solution)/shard_map/dot_general | solution.py:96
  445.6 10.7 %all-gather.11 = f32[1,2048]{1,0:T(1,128)S(1)} all-gather(f32[1,256]{1,0:T(1,128)S(1)} %get-tuple-element.59), channel_id=13, replica_groups=mesh['dp'=1,'w'=8] {'w'}, dimensions={1}, use_global_device_ids=true | all-gather | bytes 9216 | tf_op jit(solution)/shard_map/all_gather | solution.py:55
  456.4 11.2 %all-gather.6 = f32[1,2048]{1,0:T(1,128)S(1)} all-gather(f32[1,256]{1,0:T(1,128)S(1)} %get-tuple-element.61), channel_id=8, replica_groups=mesh['dp'=1,'w'=8] {'w'}, dimensions={1}, use_global_device_ids=true | all-gather | bytes 9216 | tf_op jit(solution)/shard_map/all_gather | solution.py:55
  467.6 37.6 %reduce-scatter.3.cloned.1.call-done = f32[128,2048]{1,0:T(8,128)} async-done(((f32[1024,2048]{1,0:T(8,128)}), f32[128,2048]{1,0:T(8,128)}) %reduce-scatter.3.cloned.1.call-update) | async-done | bytes 1048592 | tf_op jit(solution)/shard_map/reduce_scatter | solution.py:97
  506.7 48.8 %all-gather.35.cloned.1.call-done = bf16[1,2048,2048]{2,1,0:T(8,128)(2,1)} async-done(((bf16[1,256,2048]{2,1,0:T(8,128)(2,1)}), bf16[1,2048,2048]{2,1,0:T(8,128)(2,1)}) %all-gather.35.cloned.1.call-update) | async-done | bytes 8388624 | tf_op jit(solution)/shard_map/all_gather | solution.py:55
  555.4 4.7 fusion.36
  560.5 14.4 %all-gather.37.cloned.1.call-done = bf16[1,2048,256]{2,1,0:T(8,128)(2,1)} async-done(((bf16[1,256,256]{2,1,0:T(8,128)(2,1)}), bf16[1,2048,256]{2,1,0:T(8,128)(2,1)}) %all-gather.37.cloned.1.call-update) | async-done | bytes 1048592 | tf_op jit(solution)/shard_map/all_gather | solution.py:55
  576.8 17.5 %all-gather.39.cloned.1.call-done = bf16[1,2048,256]{2,1,0:T(8,128)(2,1)} async-done(((bf16[1,256,256]{2,1,0:T(8,128)(2,1)}), bf16[1,2048,256]{2,1,0:T(8,128)(2,1)}) %all-gather.39.cloned.1.call-update) | async-done | bytes 1048592 | tf_op jit(solution)/shard_map/all_gather | solution.py:55
  595.9 9.9 fusion.157
  605.9 8.8 fusion.2
  615.4 28.9 %all-gather.41.cloned.1.call-done = bf16[1,2048,2048]{2,1,0:T(8,128)(2,1)} async-done(((bf16[1,256,2048]{2,1,0:T(8,128)(2,1)}), bf16[1,2048,2048]{2,1,0:T(8,128)(2,1)}) %all-gather.41.cloned.1.call-update) | async-done | bytes 8388624 | tf_op jit(solution)/shard_map/all_gather | solution.py:55
  644.3 4.8 multiply_reduce_fusion
  651.1 3.9 dynamic-slice_bitcast_fusion.7
  658.7 3.8 dynamic-slice_bitcast_fusion
  662.5 4.5 broadcast.240.clone.2
  669.3 4.3 broadcast.240.clone.3
  678.4 41.9 %collective-permute-done.15 = bf16[256,2048]{1,0:T(8,128)(2,1)S(1)} collective-permute-done((bf16[256,2048]{1,0:T(8,128)(2,1)S(1)}, bf16[256,2048]{1,0:T(8,128)(2,1)S(1)}, u32[]{:S(2)}, u32[]{:S(2)}) %collective-permute-start.15) | collective-permute-done | bytes 1048608 | tf_op jit(solution)/shard_map/ppermute | solution.py:66
  727.5 16.2 %collective-permute-done.19 = bf16[256,2048]{1,0:T(8,128)(2,1)S(1)} collective-permute-done((bf16[256,2048]{1,0:T(8,128)(2,1)S(1)}, bf16[256,2048]{1,0:T(8,128)(2,1)S(1)}, u32[]{:S(2)}, u32[]{:S(2)}) %collective-permute-start.19) | collective-permute-done | bytes 1048608 | tf_op jit(solution)/shard_map/ppermute | solution.py:66
  745.3 20.8 %collective-permute-done.20 = bf16[256,2048]{1,0:T(8,128)(2,1)S(1)} collective-permute-done((bf16[256,2048]{1,0:T(8,128)(2,1)S(1)}, bf16[256,2048]{1,0:T(8,128)(2,1)S(1)}, u32[]{:S(2)}, u32[]{:S(2)}) %collective-permute-start.20) | collective-permute-done | bytes 1048608 | tf_op jit(solution)/shard_map/ppermute | solution.py:66
  770.0 17.8 %collective-permute-done.22 = bf16[256,2048]{1,0:T(8,128)(2,1)S(1)} collective-permute-done((bf16[256,2048]{1,0:T(8,128)(2,1)S(1)}, bf16[256,2048]{1,0:T(8,128)(2,1)S(1)}, u32[]{:S(2)}, u32[]{:S(2)}) %collective-permute-start.22) | collective-permute-done | bytes 1048608 | tf_op jit(solution)/shard_map/ppermute | solution.py:66
  789.9 20.2 %collective-permute-done.23 = bf16[256,2048]{1,0:T(8,128)(2,1)S(1)} collective-permute-done((bf16[256,2048]{1,0:T(8,128)(2,1)S(1)}, bf16[256,2048]{1,0:T(8,128)(2,1)S(1)}, u32[]{:S(2)}, u32[]{:S(2)}) %collective-permute-start.23) | collective-permute-done | bytes 1048608 | tf_op jit(solution)/shard_map/ppermute | solution.py:66
  813.4 20.3 %collective-permute-done.26 = bf16[256,2048]{1,0:T(8,128)(2,1)S(1)} collective-permute-done((bf16[256,2048]{1,0:T(8,128)(2,1)S(1)}, bf16[256,2048]{1,0:T(8,128)(2,1)S(1)}, u32[]{:S(2)}, u32[]{:S(2)}) %collective-permute-start.26) | collective-permute-done | bytes 1048608 | tf_op jit(solution)/shard_map/ppermute | solution.py:66
  834.7 21.3 %collective-permute-done.27 = bf16[256,2048]{1,0:T(8,128)(2,1)S(1)} collective-permute-done((bf16[256,2048]{1,0:T(8,128)(2,1)S(1)}, bf16[256,2048]{1,0:T(8,128)(2,1)S(1)}, u32[]{:S(2)}, u32[]{:S(2)}) %collective-permute-start.27) | collective-permute-done | bytes 1048608 | tf_op jit(solution)/shard_map/ppermute | solution.py:66
  857.1 14.6 %fusion.160 = f32[1024,2048]{1,0:T(8,128)} fusion(bf16[1024,2048]{1,0:T(8,128)(2,1)} %all-gather.25.cloned.1.call-done, bf16[2048,2048]{1,0:T(8,128)(2,1)} %constant_dynamic-update-slice_fusion.6), kind=kOutput, calls=%fused_computation.247 | convolution fusion | flops 8589934592 | bytes 20971520 | tf_op jit(solution)/shard_map/dot_general | solution.py:93
  871.7 31.1 %fusion.32 = f32[1024,2048]{1,0:T(8,128)} fusion(bf16[2,2048,2048]{2,1,0:T(8,128)(2,1)} %param.25, f32[1024,2048]{1,0:T(8,128)} %fusion.160, bf16[1024,2048]{1,0:T(8,128)(2,1)} %all-gather.25.cloned.1.call-done, bf16[2048,2048]{1,0:T(8,128)(2,1)} %constant_dynamic-update-slice_fusion.5), kind=kOutput, calls=%fused_computation.44 | convolution fusion | flops 17200840704 | bytes 37748736 | tf_op jit(solution)/shard_map/dot_general | solution.py:96
  903.7 33.0 %broadcast_select_fusion.1 = (bf16[1,128,1,256,256]{4,3,1,2,0:T(8,128)(2,1)}, bf16[1,128,1,256,256]{4,3,1,2,0:T(8,128)(2,1)}, bf16[1,128,1,256,256]{4,3,2,1,0:T(8,128)(2,1)}) fusion(pred[128,256]{1,0:T(8,128)(4,1)S(1)} %get-tuple-element.66, bf16[2,128,1,256,256]{4,3,1,2,0:T(8,128)(2,1)} %bitcast.195, bf16[128,256]{1,0:T(8,128)(2,1)S(1)} %copy-done.10, ...), kind=kLoop, calls=%fused_computation.15 | loop fusion | flops 25165824 | bytes 100892672 | tf_op jit(solution)/shard_map/jit(_where)/select_n | solution.py:41
  936.7 23.0 %maximum_bitcast_fusion = bf16[2,128,1,256,256]{4,3,2,1,0:T(8,128)(2,1)} fusion(bf16[1,128,1,256,256]{4,3,1,2,0:T(8,128)(2,1)} %get-tuple-element.9, bf16[1,128,1,256,256]{4,3,1,2,0:T(8,128)(2,1)} %get-tuple-element.8), kind=kLoop, calls=%fused_computation.2 | loop fusion | flops 16777216 | bytes 67108864
  959.6 11.9 %bitcast_select_fusion = bf16[1,128,1,256,256]{4,3,2,1,0:T(8,128)(2,1)} fusion(pred[128,256]{1,0:T(8,128)(4,1)S(1)} %get-tuple-element.66, bf16[2,128,1,256,256]{4,3,2,1,0:T(8,128)(2,1)} %param.16, bf16[128,256]{1,0:T(8,128)(2,1)S(1)} %convolution_convert_fusion), kind=kLoop, calls=%fused_computation.4 | loop fusion | flops 8388608 | bytes 33652736 | tf_op jit(solution)/shard_map/jit(_where)/select_n | solution.py:42
  971.5 22.9 %pad_maximum_fusion = bf16[2,128,1,256,256]{4,3,2,1,0:T(8,128)(2,1)} fusion(bf16[1,128,1,256,256]{4,3,2,1,0:T(8,128)(2,1)} %bitcast_select_fusion, bf16[1,128,1,256,256]{4,3,2,1,0:T(8,128)(2,1)} %get-tuple-element.58), kind=kLoop, calls=%fused_computation.3 | loop fusion | flops 16777216 | bytes 67108864 | tf_op jit(solution)/shard_map/stack | solution.py:101
  (194 shorter events, 110.3 us)
Async XLA Ops:
  7.2 50.4 %all-gather.29.cloned.1.call-start = ((), (), s32[]{:S(2)}) async-start(), calls=%async_computation.7 | async-start | bytes 1179648 | tf_op jit(solution)/shard_map/all_gather | solution.py:55
  8.9 50.7 %all-gather.31.cloned.1.call-start = ((), (), s32[]{:S(2)}) async-start(), calls=%async_computation.8 | async-start | bytes 1179648 | tf_op jit(solution)/shard_map/all_gather | solution.py:55
  10.7 90.3 %all-gather.27.cloned.1.call-start = ((), (), s32[]{:S(2)}) async-start(), calls=%async_computation.6 | async-start | bytes 9437184 | tf_op jit(solution)/shard_map/all_gather | solution.py:55
  13.9 137.3 %all-gather.33.cloned.1.call-start = ((), (), s32[]{:S(2)}) async-start(), calls=%async_computation.9 | async-start | bytes 9437184 | tf_op jit(solution)/shard_map/all_gather | solution.py:55
  17.1 379.7 %all-gather.23.cloned.1.call-start = ((), (), s32[]{:S(2)}) async-start(), calls=%async_computation.2 | async-start | bytes 4718592 | tf_op jit(solution)/shard_map/all_gather | solution.py:55
  26.5 30.4 %copy-start.4 = (bf16[128,2048]{1,0:T(8,128)(2,1)S(1)}, bf16[128,2048]{1,0:T(8,128)(2,1)}, u32[]{:S(2)}) copy-start(bf16[128,2048]{1,0:T(8,128)(2,1)} %param.13) | copy-start | bytes 1572868
  32.5 157.3 %collective-permute-start = (bf16[256,2048]{1,0:T(8,128)(2,1)}, bf16[256,2048]{1,0:T(8,128)(2,1)}, u32[]{:S(2)}, u32[]{:S(2)}) collective-permute-start(bf16[256,2048]{1,0:T(8,128)(2,1)} %get-tuple-element.34), channel_id=1, source_target_pairs={{0,1},{1,0},{2,3},{3,2},{4,5},{5,4},{6,7},{7,6}} | collective-permute-start | bytes 3145736 | tf_op jit(solution)/shard_map/ppermute | solution.py:66
  59.5 46.8 %copy-start.9 = (bf16[128,256]{1,0:T(8,128)(2,1)}, bf16[128,256]{1,0:T(8,128)(2,1)S(1)}, u32[]{:S(2)}) copy-start(bf16[128,256]{1,0:T(8,128)(2,1)S(1)} %pad_maximum_fusion.1) | copy-start | bytes 196612
  61.2 55.4 %copy-start.11 = (bf16[128,256]{1,0:T(8,128)(2,1)}, bf16[128,256]{1,0:T(8,128)(2,1)S(1)}, u32[]{:S(2)}) copy-start(bf16[128,256]{1,0:T(8,128)(2,1)S(1)} %convolution_convert_fusion.1) | copy-start | bytes 196612
  157.0 348.3 %reduce-scatter.3.cloned.1.call-start = ((), (), s32[]{:S(2)}) async-start(), calls=%async_computation.3 | async-start | bytes 9437184 | tf_op jit(solution)/shard_map/reduce_scatter | solution.py:97
  173.0 19.9 %collective-permute-start.7 = (bf16[256,2048]{1,0:T(8,128)(2,1)}, bf16[256,2048]{1,0:T(8,128)(2,1)}, u32[]{:S(2)}, u32[]{:S(2)}) collective-permute-start(bf16[256,2048]{1,0:T(8,128)(2,1)} %get-tuple-element.41), channel_id=1, source_target_pairs={{0,1},{1,0},{2,3},{3,2},{4,5},{5,4},{6,7},{7,6}} | collective-permute-start | bytes 3145736 | tf_op jit(solution)/shard_map/ppermute | solution.py:66
  173.3 35.7 %collective-permute-start.1 = (bf16[256,2048]{1,0:T(8,128)(2,1)}, bf16[256,2048]{1,0:T(8,128)(2,1)}, u32[]{:S(2)}, u32[]{:S(2)}) collective-permute-start(bf16[256,2048]{1,0:T(8,128)(2,1)} %get-tuple-element.33), channel_id=1, source_target_pairs={{0,2},{1,3},{2,0},{3,1},{4,6},{5,7},{6,4},{7,5}} | collective-permute-start | bytes 3145736 | tf_op jit(solution)/shard_map/ppermute | solution.py:66
  174.7 82.4 %collective-permute-start.2 = (bf16[256,2048]{1,0:T(8,128)(2,1)}, bf16[256,2048]{1,0:T(8,128)(2,1)}, u32[]{:S(2)}, u32[]{:S(2)}) collective-permute-start(bf16[256,2048]{1,0:T(8,128)(2,1)} %get-tuple-element.32), channel_id=1, source_target_pairs={{0,3},{1,2},{2,1},{3,0},{4,7},{5,6},{6,5},{7,4}} | collective-permute-start | bytes 3145736 | tf_op jit(solution)/shard_map/ppermute | solution.py:66
  174.9 79.1 %collective-permute-start.8 = (bf16[256,2048]{1,0:T(8,128)(2,1)}, bf16[256,2048]{1,0:T(8,128)(2,1)}, u32[]{:S(2)}, u32[]{:S(2)}) collective-permute-start(bf16[256,2048]{1,0:T(8,128)(2,1)} %get-tuple-element.40), channel_id=1, source_target_pairs={{0,2},{1,3},{2,0},{3,1},{4,6},{5,7},{6,4},{7,5}} | collective-permute-start | bytes 3145736 | tf_op jit(solution)/shard_map/ppermute | solution.py:66
  187.4 88.5 %copy-start.5 = (bf16[256,2048]{1,0:T(8,128)(2,1)S(1)}, bf16[256,2048]{1,0:T(8,128)(2,1)}, u32[]{:S(2)}) copy-start(bf16[256,2048]{1,0:T(8,128)(2,1)} %get-tuple-element.29) | copy-start | bytes 3145732
  189.9 67.2 %copy-start.8 = (bf16[256,2048]{1,0:T(8,128)(2,1)S(1)}, bf16[256,2048]{1,0:T(8,128)(2,1)}, u32[]{:S(2)}) copy-start(bf16[256,2048]{1,0:T(8,128)(2,1)} %get-tuple-element.37) | copy-start | bytes 3145732
  189.9 88.6 %copy-start.7 = (bf16[256,2048]{1,0:T(8,128)(2,1)S(1)}, bf16[256,2048]{1,0:T(8,128)(2,1)}, u32[]{:S(2)}) copy-start(bf16[256,2048]{1,0:T(8,128)(2,1)} %get-tuple-element.36) | copy-start | bytes 3145732
  189.9 93.0 %copy-start.6 = (bf16[256,2048]{1,0:T(8,128)(2,1)S(1)}, bf16[256,2048]{1,0:T(8,128)(2,1)}, u32[]{:S(2)}) copy-start(bf16[256,2048]{1,0:T(8,128)(2,1)} %get-tuple-element.35) | copy-start | bytes 3145732
  189.9 86.0 %collective-permute-start.9 = (bf16[256,2048]{1,0:T(8,128)(2,1)}, bf16[256,2048]{1,0:T(8,128)(2,1)S(1)}, u32[]{:S(2)}, u32[]{:S(2)}) collective-permute-start(bf16[256,2048]{1,0:T(8,128)(2,1)} %get-tuple-element.39), channel_id=1, source_target_pairs={{0,3},{1,2},{2,1},{3,0},{4,7},{5,6},{6,5},{7,4}} | collective-permute-start | bytes 3145736 | tf_op jit(solution)/shard_map/ppermute | solution.py:66
  192.9 85.5 %collective-permute-start.3 = (bf16[256,2048]{1,0:T(8,128)(2,1)}, bf16[256,2048]{1,0:T(8,128)(2,1)S(1)}, u32[]{:S(2)}, u32[]{:S(2)}) collective-permute-start(bf16[256,2048]{1,0:T(8,128)(2,1)} %get-tuple-element.31), channel_id=1, source_target_pairs={{0,4},{1,5},{2,6},{3,7},{4,0},{5,1},{6,2},{7,3}} | collective-permute-start | bytes 3145736 | tf_op jit(solution)/shard_map/ppermute | solution.py:66
  209.0 71.9 %collective-permute-start.10 = (bf16[256,2048]{1,0:T(8,128)(2,1)}, bf16[256,2048]{1,0:T(8,128)(2,1)S(1)}, u32[]{:S(2)}, u32[]{:S(2)}) collective-permute-start(bf16[256,2048]{1,0:T(8,128)(2,1)} %get-tuple-element.38), channel_id=1, source_target_pairs={{0,4},{1,5},{2,6},{3,7},{4,0},{5,1},{6,2},{7,3}} | collective-permute-start | bytes 3145736 | tf_op jit(solution)/shard_map/ppermute | solution.py:66
  253.9 28.9 %collective-permute-start.4 = (bf16[256,2048]{1,0:T(8,128)(2,1)}, bf16[256,2048]{1,0:T(8,128)(2,1)S(1)}, u32[]{:S(2)}, u32[]{:S(2)}) collective-permute-start(bf16[256,2048]{1,0:T(8,128)(2,1)} %get-tuple-element.30), channel_id=1, source_target_pairs={{0,5},{1,4},{2,7},{3,6},{4,1},{5,0},{6,3},{7,2}} | collective-permute-start | bytes 3145736 | tf_op jit(solution)/shard_map/ppermute | solution.py:66
  257.1 134.4 %collective-permute-start.11 = (bf16[256,2048]{1,0:T(8,128)(2,1)S(1)}, bf16[256,2048]{1,0:T(8,128)(2,1)S(1)}, u32[]{:S(2)}, u32[]{:S(2)}) collective-permute-start(bf16[256,2048]{1,0:T(8,128)(2,1)S(1)} %copy-done.8), channel_id=1, source_target_pairs={{0,5},{1,4},{2,7},{3,6},{4,1},{5,0},{6,3},{7,2}} | collective-permute-start | bytes 3145736 | tf_op jit(solution)/shard_map/ppermute | solution.py:66
  275.9 116.6 %collective-permute-start.5 = (bf16[256,2048]{1,0:T(8,128)(2,1)S(1)}, bf16[256,2048]{1,0:T(8,128)(2,1)S(1)}, u32[]{:S(2)}, u32[]{:S(2)}) collective-permute-start(bf16[256,2048]{1,0:T(8,128)(2,1)S(1)} %copy-done.5), channel_id=1, source_target_pairs={{0,6},{1,7},{2,4},{3,5},{4,2},{5,3},{6,0},{7,1}} | collective-permute-start | bytes 3145736 | tf_op jit(solution)/shard_map/ppermute | solution.py:66
  278.5 115.1 %collective-permute-start.12 = (bf16[256,2048]{1,0:T(8,128)(2,1)S(1)}, bf16[256,2048]{1,0:T(8,128)(2,1)S(1)}, u32[]{:S(2)}, u32[]{:S(2)}) collective-permute-start(bf16[256,2048]{1,0:T(8,128)(2,1)S(1)} %copy-done.7), channel_id=1, source_target_pairs={{0,6},{1,7},{2,4},{3,5},{4,2},{5,3},{6,0},{7,1}} | collective-permute-start | bytes 3145736 | tf_op jit(solution)/shard_map/ppermute | solution.py:66
  280.9 113.7 %collective-permute-start.6 = (bf16[256,2048]{1,0:T(8,128)(2,1)S(1)}, bf16[256,2048]{1,0:T(8,128)(2,1)S(1)}, u32[]{:S(2)}, u32[]{:S(2)}) collective-permute-start(bf16[256,2048]{1,0:T(8,128)(2,1)S(1)} %get-tuple-element.28), channel_id=1, source_target_pairs={{0,7},{1,6},{2,5},{3,4},{4,3},{5,2},{6,1},{7,0}} | collective-permute-start | bytes 3145736 | tf_op jit(solution)/shard_map/ppermute | solution.py:66
  282.8 112.8 %collective-permute-start.13 = (bf16[256,2048]{1,0:T(8,128)(2,1)S(1)}, bf16[256,2048]{1,0:T(8,128)(2,1)S(1)}, u32[]{:S(2)}, u32[]{:S(2)}) collective-permute-start(bf16[256,2048]{1,0:T(8,128)(2,1)S(1)} %copy-done.6), channel_id=1, source_target_pairs={{0,7},{1,6},{2,5},{3,4},{4,3},{5,2},{6,1},{7,0}} | collective-permute-start | bytes 3145736 | tf_op jit(solution)/shard_map/ppermute | solution.py:66
  442.8 112.7 %all-gather.35.cloned.1.call-start = ((), (), s32[]{:S(2)}) async-start(), calls=%async_computation.10 | async-start | bytes 9437184 | tf_op jit(solution)/shard_map/all_gather | solution.py:55
  443.5 131.3 %all-gather.37.cloned.1.call-start = ((), (), s32[]{:S(2)}) async-start(), calls=%async_computation.11 | async-start | bytes 1179648 | tf_op jit(solution)/shard_map/all_gather | solution.py:55
  444.3 150.0 %all-gather.39.cloned.1.call-start = ((), (), s32[]{:S(2)}) async-start(), calls=%async_computation.12 | async-start | bytes 1179648 | tf_op jit(solution)/shard_map/all_gather | solution.py:55
  445.0 199.3 %all-gather.41.cloned.1.call-start = ((), (), s32[]{:S(2)}) async-start(), calls=%async_computation.13 | async-start | bytes 9437184 | tf_op jit(solution)/shard_map/all_gather | solution.py:55
  445.6 411.5 %all-gather.25.cloned.1.call-start = ((), (), s32[]{:S(2)}) async-start(), calls=%async_computation.4 | async-start | bytes 4718592 | tf_op jit(solution)/shard_map/all_gather | solution.py:55
  651.0 343.4 %reduce-scatter.5.cloned.1.call-start = ((), (), s32[]{:S(2)}) async-start(), calls=%async_computation.5 | async-start | bytes 9437184 | tf_op jit(solution)/shard_map/reduce_scatter | solution.py:97
  654.9 21.0 %collective-permute-start.14 = (bf16[256,2048]{1,0:T(8,128)(2,1)S(1)}, bf16[256,2048]{1,0:T(8,128)(2,1)S(1)}, u32[]{:S(2)}, u32[]{:S(2)}) collective-permute-start(bf16[256,2048]{1,0:T(8,128)(2,1)S(1)} %get-tuple-element.20), channel_id=1, source_target_pairs={{0,1},{1,0},{2,3},{3,2},{4,5},{5,4},{6,7},{7,6}} | collective-permute-start | bytes 3145736 | tf_op jit(solution)/shard_map/ppermute | solution.py:66
  655.2 71.3 %collective-permute-start.18 = (bf16[256,2048]{1,0:T(8,128)(2,1)S(1)}, bf16[256,2048]{1,0:T(8,128)(2,1)S(1)}, u32[]{:S(2)}, u32[]{:S(2)}) collective-permute-start(bf16[256,2048]{1,0:T(8,128)(2,1)S(1)} %get-tuple-element.16), channel_id=1, source_target_pairs={{0,5},{1,4},{2,7},{3,6},{4,1},{5,0},{6,3},{7,2}} | collective-permute-start | bytes 3145736 | tf_op jit(solution)/shard_map/ppermute | solution.py:66
  656.2 67.8 %collective-permute-start.17 = (bf16[256,2048]{1,0:T(8,128)(2,1)S(1)}, bf16[256,2048]{1,0:T(8,128)(2,1)S(1)}, u32[]{:S(2)}, u32[]{:S(2)}) collective-permute-start(bf16[256,2048]{1,0:T(8,128)(2,1)S(1)} %get-tuple-element.17), channel_id=1, source_target_pairs={{0,4},{1,5},{2,6},{3,7},{4,0},{5,1},{6,2},{7,3}} | collective-permute-start | bytes 3145736 | tf_op jit(solution)/shard_map/ppermute | solution.py:66
  657.1 65.4 %collective-permute-start.16 = (bf16[256,2048]{1,0:T(8,128)(2,1)S(1)}, bf16[256,2048]{1,0:T(8,128)(2,1)S(1)}, u32[]{:S(2)}, u32[]{:S(2)}) collective-permute-start(bf16[256,2048]{1,0:T(8,128)(2,1)S(1)} %get-tuple-element.18), channel_id=1, source_target_pairs={{0,3},{1,2},{2,1},{3,0},{4,7},{5,6},{6,5},{7,4}} | collective-permute-start | bytes 3145736 | tf_op jit(solution)/shard_map/ppermute | solution.py:66
  658.1 62.2 %collective-permute-start.15 = (bf16[256,2048]{1,0:T(8,128)(2,1)S(1)}, bf16[256,2048]{1,0:T(8,128)(2,1)S(1)}, u32[]{:S(2)}, u32[]{:S(2)}) collective-permute-start(bf16[256,2048]{1,0:T(8,128)(2,1)S(1)} %get-tuple-element.19), channel_id=1, source_target_pairs={{0,2},{1,3},{2,0},{3,1},{4,6},{5,7},{6,4},{7,5}} | collective-permute-start | bytes 3145736 | tf_op jit(solution)/shard_map/ppermute | solution.py:66
  675.9 67.8 %collective-permute-start.19 = (bf16[256,2048]{1,0:T(8,128)(2,1)S(1)}, bf16[256,2048]{1,0:T(8,128)(2,1)S(1)}, u32[]{:S(2)}, u32[]{:S(2)}) collective-permute-start(bf16[256,2048]{1,0:T(8,128)(2,1)S(1)} %get-tuple-element.15), channel_id=1, source_target_pairs={{0,6},{1,7},{2,4},{3,5},{4,2},{5,3},{6,0},{7,1}} | collective-permute-start | bytes 3145736 | tf_op jit(solution)/shard_map/ppermute | solution.py:66
  720.3 45.8 %collective-permute-start.20 = (bf16[256,2048]{1,0:T(8,128)(2,1)S(1)}, bf16[256,2048]{1,0:T(8,128)(2,1)S(1)}, u32[]{:S(2)}, u32[]{:S(2)}) collective-permute-start(bf16[256,2048]{1,0:T(8,128)(2,1)S(1)} %get-tuple-element.14), channel_id=1, source_target_pairs={{0,7},{1,6},{2,5},{3,4},{4,3},{5,2},{6,1},{7,0}} | collective-permute-start | bytes 3145736 | tf_op jit(solution)/shard_map/ppermute | solution.py:66
  722.5 45.0 %collective-permute-start.21 = (bf16[256,2048]{1,0:T(8,128)(2,1)S(1)}, bf16[256,2048]{1,0:T(8,128)(2,1)S(1)}, u32[]{:S(2)}, u32[]{:S(2)}) collective-permute-start(bf16[256,2048]{1,0:T(8,128)(2,1)S(1)} %get-tuple-element.27), channel_id=1, source_target_pairs={{0,1},{1,0},{2,3},{3,2},{4,5},{5,4},{6,7},{7,6}} | collective-permute-start | bytes 3145736 | tf_op jit(solution)/shard_map/ppermute | solution.py:66
  724.0 63.8 %collective-permute-start.22 = (bf16[256,2048]{1,0:T(8,128)(2,1)S(1)}, bf16[256,2048]{1,0:T(8,128)(2,1)S(1)}, u32[]{:S(2)}, u32[]{:S(2)}) collective-permute-start(bf16[256,2048]{1,0:T(8,128)(2,1)S(1)} %get-tuple-element.26), channel_id=1, source_target_pairs={{0,2},{1,3},{2,0},{3,1},{4,6},{5,7},{6,4},{7,5}} | collective-permute-start | bytes 3145736 | tf_op jit(solution)/shard_map/ppermute | solution.py:66
  726.5 83.7 %collective-permute-start.23 = (bf16[256,2048]{1,0:T(8,128)(2,1)S(1)}, bf16[256,2048]{1,0:T(8,128)(2,1)S(1)}, u32[]{:S(2)}, u32[]{:S(2)}) collective-permute-start(bf16[256,2048]{1,0:T(8,128)(2,1)S(1)} %get-tuple-element.25), channel_id=1, source_target_pairs={{0,3},{1,2},{2,1},{3,0},{4,7},{5,6},{6,5},{7,4}} | collective-permute-start | bytes 3145736 | tf_op jit(solution)/shard_map/ppermute | solution.py:66
  743.7 67.6 %collective-permute-start.24 = (bf16[256,2048]{1,0:T(8,128)(2,1)S(1)}, bf16[256,2048]{1,0:T(8,128)(2,1)S(1)}, u32[]{:S(2)}, u32[]{:S(2)}) collective-permute-start(bf16[256,2048]{1,0:T(8,128)(2,1)S(1)} %get-tuple-element.24), channel_id=1, source_target_pairs={{0,4},{1,5},{2,6},{3,7},{4,0},{5,1},{6,2},{7,3}} | collective-permute-start | bytes 3145736 | tf_op jit(solution)/shard_map/ppermute | solution.py:66
  766.1 46.2 %collective-permute-start.25 = (bf16[256,2048]{1,0:T(8,128)(2,1)S(1)}, bf16[256,2048]{1,0:T(8,128)(2,1)S(1)}, u32[]{:S(2)}, u32[]{:S(2)}) collective-permute-start(bf16[256,2048]{1,0:T(8,128)(2,1)S(1)} %get-tuple-element.23), channel_id=1, source_target_pairs={{0,5},{1,4},{2,7},{3,6},{4,1},{5,0},{6,3},{7,2}} | collective-permute-start | bytes 3145736 | tf_op jit(solution)/shard_map/ppermute | solution.py:66
  767.5 66.2 %collective-permute-start.26 = (bf16[256,2048]{1,0:T(8,128)(2,1)S(1)}, bf16[256,2048]{1,0:T(8,128)(2,1)S(1)}, u32[]{:S(2)}, u32[]{:S(2)}) collective-permute-start(bf16[256,2048]{1,0:T(8,128)(2,1)S(1)} %get-tuple-element.22), channel_id=1, source_target_pairs={{0,6},{1,7},{2,4},{3,5},{4,2},{5,3},{6,0},{7,1}} | collective-permute-start | bytes 3145736 | tf_op jit(solution)/shard_map/ppermute | solution.py:66
  787.8 68.2 %collective-permute-start.27 = (bf16[256,2048]{1,0:T(8,128)(2,1)S(1)}, bf16[256,2048]{1,0:T(8,128)(2,1)S(1)}, u32[]{:S(2)}, u32[]{:S(2)}) collective-permute-start(bf16[256,2048]{1,0:T(8,128)(2,1)S(1)} %get-tuple-element.21), channel_id=1, source_target_pairs={{0,7},{1,6},{2,5},{3,4},{4,3},{5,2},{6,1},{7,0}} | collective-permute-start | bytes 3145736 | tf_op jit(solution)/shard_map/ppermute | solution.py:66
  971.5 22.9 %copy-start.3 = (f32[128,2048]{1,0:T(8,128)S(1)}, f32[128,2048]{1,0:T(8,128)}, u32[]{:S(2)}) copy-start(f32[128,2048]{1,0:T(8,128)} %copy-done.2) | copy-start | bytes 3145732
  (16 other events, 140.2 us)
Sparse Core Ops, SparseCore 0:
  9.8 20.3 all-gather.28
  32.6 17.6 all-gather.30
  52.7 48.3 all-gather.26
  102.7 48.4 all-gather.32
  157.1 40.9 all-gather.22
  442.9 62.3 reduce-scatter.2
  507.1 48.3 all-gather.34
  557.3 17.5 all-gather.36
  576.7 17.5 all-gather.38
  595.9 48.3 all-gather.40
  651.1 48.2 all-gather.24
  903.0 61.3 reduce-scatter.4

commit v2 on v0

v2 whole, which is shorter than its diff:
```python
import functools

import jax
import jax.numpy as jnp
from jax import lax
from jax.experimental import pallas as pl
from jax.experimental.pallas import tpu as pltpu
from jax.sharding import PartitionSpec as P

EPS = 1e-6
ROPE_BASE = 10000.0
MESH = pl.DeviceIdType.MESH
BF16 = jnp.bfloat16
F32 = jnp.float32

WAYS = 8
LAYERS = 2
ROWS = 128
BATCH = ROWS * WAYS
D = 2048
SHARD = D // WAYS
HEADS = 8
HEAD = 256
HALF = HEAD // 2
SMAX = 256
FF_BLOCK = 2048
CHUNK = 256
CHUNKS = FF_BLOCK // CHUNK
GROUP = 8
GROUPS = ROWS // GROUP
SUB = 512
PEERS = (6, 7, 2, 4, 3, 5, 1)
AHEAD = 3


def rope_tables(positions):
    inv_freq = ROPE_BASE ** (-2.0 * jnp.arange(HALF, dtype=F32) / HEAD)
    angles = positions.astype(F32)[:, None] * inv_freq[None, :]
    return jnp.cos(angles), jnp.sin(angles)


def al(index, size):
    return pl.ds(pl.multiple_of(index * size, size), size)


def layers_kernel(hid_in, pos_rep, cos_ref, sin_ref, gains_own, k_cache, v_cache,
                  wq, wk, wv, wo, qx, kx, vx, ox, qy, ky, vy, oy, w_gate, w_up, w_down,
                  hid_out, kn_out, vn_out, qbuf, kbuf, vbuf, obuf, gbuf, ubuf,
                  gains_all, hid, x_act, q_head, q_seq, a_seq, a_flat, kn, vn, kv_k, kv_v, w_tile,
                  y_full, g_tile, u_tile, d_tile, m_act, acc, core_recv, p1a, p1b, p2a, p2b,
                  gain_s, gain_r, fwd_s, fwd_r, rel_s, rel_r, chunk_s, chunk_r, y_s, y_r,
                  rs_s, rs_r, tile_sem, kv_sem, gate_sem, down_sem):
    me = lax.axis_index("w")
    core = lax.rem(me, 2)
    xbit = lax.rem(me // 2, 2)
    ybit = me // 4
    peer = [jnp.bitwise_xor(me, m) for m in range(WAYS)]

    def send(src, dst, m, ssem, rsem):
        return pltpu.make_async_remote_copy(src_ref=src, dst_ref=dst, send_sem=ssem, recv_sem=rsem,
                                            device_id={"w": peer[m]}, device_id_type=MESH)

    barrier = pltpu.get_barrier_semaphore()
    for m in range(1, WAYS):
        pl.semaphore_signal(barrier, inc=1, device_id={"w": peer[m]}, device_id_type=MESH)
    pl.semaphore_wait(barrier, WAYS - 1)

    gain_copies = [send(gains_own, gains_all.at[me], m, gain_s.at[m], gain_r.at[m]) for m in range(1, WAYS)]
    for c in gain_copies:
        c.start()
    gains_all[me] = gains_own[...]

    own = (wq, wk, wv, wo)
    from_x = (qx, kx, vx, ox)
    from_y = (qy, ky, vy, oy)
    bufs = (qbuf, kbuf, vbuf, obuf)
    half = SHARD // 2

    def forwards(l, a):
        return (send(from_x[a].at[l, pl.ds(0, half)], bufs[a].at[l, 6, pl.ds(0, half)], 4, fwd_s.at[l, a, 0], fwd_r.at[l, a, 0]),
                send(from_y[a].at[l, pl.ds(half, half)], bufs[a].at[l, 6, pl.ds(half, half)], 2, fwd_s.at[l, a, 1], fwd_r.at[l, a, 1]))

    def relays(l, a):
        srcs = (own[a].at[l], from_x[a].at[l], from_y[a].at[l], bufs[a].at[l, 6])
        return [send(srcs[i], bufs[a].at[l, 2 * i + 1], 1, rel_s.at[l, a, i], rel_r.at[l, a, i]) for i in range(4)]

    def weights_start(l, a):
        for c in forwards(l, a):
            c.start()
        for c in relays(l, a)[:3]:
            c.start()

    def weights_relay_last(l, a):
        for c in forwards(l, a):
            c.wait_recv()
        relays(l, a)[3].start()

    def weights_arrived(l, a):
        for c in relays(l, a):
            c.wait_recv()

    def chunk_start(g):
        l, k = g // CHUNKS, lax.rem(g, CHUNKS)
        for m in PEERS:
            cols = pl.ds(pl.multiple_of(peer[m] * FF_BLOCK + k * CHUNK, CHUNK), CHUNK)
            send(w_gate.at[l, :, cols], gbuf.at[l, k, al(me, SHARD)], m, chunk_s.at[g, 0], chunk_r.at[g, 0]).start()
            send(w_up.at[l, :, cols], ubuf.at[l, k, al(me, SHARD)], m, chunk_s.at[g, 1], chunk_r.at[g, 1]).start()

    def chunk_wait(sem, g):
        l, k = g // CHUNKS, lax.rem(g, CHUNKS)
        part = pl.ds(0, (WAYS - 1) * SHARD)
        pltpu.make_async_copy(gbuf.at[l, k, part], gbuf.at[l, k, part], sem.at[g, 0]).wait()
        pltpu.make_async_copy(ubuf.at[l, k, part], ubuf.at[l, k, part], sem.at[g, 1]).wait()

    for a in range(4):
        weights_start(0, a)

    @pl.loop(0, AHEAD)
    def _(g):
        chunk_start(g)

    for c in gain_copies:
        c.wait_recv()

    def norm_into(src, gain_row, dst, dst_row0):
        @pl.loop(0, ROWS // 32)
        def _(i):
            h = src[al(i, 32), :].astype(F32)
            r = lax.rsqrt(jnp.mean(h * h, axis=-1, keepdims=True) + EPS)
            for s in range(WAYS):
                cols = pl.ds(s * SHARD, SHARD)
                g = 1.0 + gains_all[s, pl.ds(gain_row, 1), :]
                dst[pl.ds(pl.multiple_of(dst_row0 + i * 32, 32), 32), cols] = (h[:, s * SHARD:(s + 1) * SHARD] * r * g).astype(BF16)

    def tile_copies(l, a, n, slot):
        cols = al(n, HEAD)
        srcs = (own[a].at[l], bufs[a].at[l, 1], from_x[a].at[l], bufs[a].at[l, 3],
                from_y[a].at[l], bufs[a].at[l, 5], bufs[a].at[l, 6], bufs[a].at[l, 7])
        return [pltpu.make_async_copy(srcs[m].at[:, cols], w_tile.at[slot, al(peer[m], SHARD)], tile_sem.at[slot])
                for m in range(WAYS)]

    def tile_start(l, a, n, slot):
        for c in tile_copies(l, a, n, slot):
            c.start()

    def tile_wait(slot):
        pltpu.make_async_copy(w_tile.at[slot], w_tile.at[slot], tile_sem.at[slot]).wait()

    def rope(vec):
        lead, tail = vec[:, :HALF], vec[:, HALF:]
        cos_b, sin_b = cos_ref[...], sin_ref[...]
        return jnp.concatenate([lead * cos_b - tail * sin_b, tail * cos_b + lead * sin_b], axis=-1)

    def kv_copies(l, i, slot):
        return (pltpu.make_async_copy(k_cache.at[l, al(i, GROUP)], kv_k.at[slot], kv_sem.at[slot, 0]),
                pltpu.make_async_copy(v_cache.at[l, al(i, GROUP)], kv_v.at[slot], kv_sem.at[slot, 1]))

    def kv_start(l, i, slot):
        for c in kv_copies(l, i, slot):
            c.start()

    def attention_step(l, i):
        slot = lax.rem(i, 2)

        @pl.when(i + 1 < GROUPS)
        def _():
            kv_start(l, i + 1, 1 - slot)

        for c in kv_copies(l, i, slot):
            c.wait()
        rows = GROUP * HEADS
        q64 = q_seq[al(i, GROUP)].reshape(rows, HEAD)
        kn64 = jnp.broadcast_to(kn[al(i, GROUP), :][:, None, :], (GROUP, HEADS, HEAD)).reshape(rows, HEAD)
        vn64 = jnp.broadcast_to(vn[al(i, GROUP), :][:, None, :], (GROUP, HEADS, HEAD)).reshape(rows, HEAD)
        pos = pos_rep[al(i, rows), :]
        scores = jnp.concatenate(
            [lax.dot_general(q64[s * HEADS:(s + 1) * HEADS].astype(BF16), kv_k[slot, s], (((1,), (1,)), ((), ())), preferred_element_type=F32)
             for s in range(GROUP)], axis=0)
        new_score = jnp.sum(q64 * kn64, axis=-1, keepdims=True)
        place = lax.broadcasted_iota(jnp.int32, (rows, SMAX), 1)
        is_new = place == pos
        scores = jnp.where(is_new, new_score, scores)
        scores = jnp.where(place <= pos, scores, -1e30)
        u = jnp.exp(scores - jnp.max(scores, axis=-1, keepdims=True))
        den = jnp.sum(u, axis=-1, keepdims=True)
        u_new = jnp.sum(jnp.where(is_new, u, 0.0), axis=-1, keepdims=True).astype(BF16).astype(F32)
        u_old = jnp.where(is_new, 0.0, u)
        vals = jnp.concatenate(
            [jnp.dot(u_old[s * HEADS:(s + 1) * HEADS].astype(BF16), kv_v[slot, s], preferred_element_type=F32)
             for s in range(GROUP)], axis=0)
        vals = (vals + u_new * vn64) / den
        a_seq[al(i, GROUP)] = vals.reshape(GROUP, HEADS, HEAD)

    def y_sends(l):
        mine = y_full.at[l, al(me, ROWS)]
        return {m: send(mine, mine, m, y_s.at[l, m], y_r.at[l, m]) for m in (6, 2, 4, 1)}

    def y_relay(l, m):
        block = y_full.at[l, al(peer[m], ROWS)]
        return send(block, block, 1, y_s.at[l, m + 1], y_r.at[l, m + 1])

    def chunk_tiles(l, k):
        copies = []
        own_cols = pl.ds(pl.multiple_of(me * FF_BLOCK + k * CHUNK, CHUNK), CHUNK)
        for w_own, buf, tile, s in ((w_gate, gbuf, g_tile, 0), (w_up, ubuf, u_tile, 1)):
            for m in range(WAYS):
                src = w_own.at[l, :, own_cols] if m == 0 else buf.at[l, k, al(peer[m], SHARD)]
                copies.append(pltpu.make_async_copy(src, tile.at[al(peer[m], SHARD)], gate_sem.at[s]))
        return copies

    def mlp_chunk(l, k, down):
        g = l * CHUNKS + k
        d_copy = pltpu.make_async_copy(w_down.at[l, al(k, CHUNK)], d_tile, down_sem.at[0])
        d_copy.start()
        chunk_wait(chunk_r, g)
        for c in chunk_tiles(l, k):
            c.start()
        pltpu.make_async_copy(g_tile, g_tile, gate_sem.at[0]).wait()
        pltpu.make_async_copy(u_tile, u_tile, gate_sem.at[1]).wait()

        @pl.loop(0, BATCH // 256)
        def _(i):
            y = y_full[l, al(i, 256), :]
            gate = jnp.dot(y, g_tile[...], preferred_element_type=F32)
            up = jnp.dot(y, u_tile[...], preferred_element_type=F32)
            m_act[al(i, 256), :] = (jax.nn.gelu(gate, approximate=True) * up).astype(BF16)

        d_copy.wait()
        down()

    def down_piece(s, first):
        cols = pl.ds(s * SUB, SUB) if isinstance(s, int) else al(s, SUB)

        @pl.loop(0, BATCH // 256)
        def _(i):
            part = jnp.dot(m_act[al(i, 256), :], d_tile[:, cols], preferred_element_type=F32)
            for b in range(256 // ROWS):
                blk = i * (256 // ROWS) + b
                piece = part[b * ROWS:(b + 1) * ROWS]
                acc[blk, :, cols] = piece if first else acc[blk, :, cols] + piece

    def rs_core(s):
        cols = pl.ds(s * SUB, SUB)
        return [send(acc.at[2 * j + 1 - core, :, cols], core_recv.at[j, :, cols], 1, rs_s.at[0, s, j], rs_r.at[0, s, j]) for j in range(4)]

    def rs_first(s):
        cols = pl.ds(s * SUB, SUB)
        if s < 2:
            return [send(acc.at[2 * (2 * t + 1 - xbit) + core, :, cols], p1a.at[t, :, cols], 2, rs_s.at[1, s, t], rs_r.at[1, s, t]) for t in range(2)]
        local = pl.ds((s - 2) * SUB, SUB)
        return [send(acc.at[2 * (2 * (1 - ybit) + t) + core, :, cols], p1b.at[t, :, local], 4, rs_s.at[1, s, t], rs_r.at[1, s, t]) for t in range(2)]

    def rs_second(s):
        cols = pl.ds(s * SUB, SUB)
        if s < 2:
            return [send(acc.at[2 * (2 * (1 - ybit) + xbit) + core, :, cols], p2a.at[:, cols], 4, rs_s.at[2, s, 0], rs_r.at[2, s, 0])]
        local = pl.ds((s - 2) * SUB, SUB)
        return [send(acc.at[2 * (2 * ybit + 1 - xbit) + core, :, cols], p2b.at[:, local], 2, rs_s.at[2, s, 0], rs_r.at[2, s, 0])]

    def rs_core_add(s):
        cols = pl.ds(s * SUB, SUB)
        for c in rs_core(s):
            c.wait_recv()

        @pl.loop(0, 4)
        def _(j):
            acc[2 * j + core, :, cols] = acc[2 * j + core, :, cols] + core_recv[j, :, cols]

    def rs_first_add(s):
        cols = pl.ds(s * SUB, SUB)
        for c in rs_first(s):
            c.wait_recv()

        @pl.loop(0, 2)
        def _(t):
            if s < 2:
                blk = 2 * (2 * t + xbit) + core
                acc[blk, :, cols] = acc[blk, :, cols] + p1a[t, :, cols]
            else:
                blk = 2 * (2 * ybit + t) + core
                acc[blk, :, cols] = acc[blk, :, cols] + p1b[t, :, pl.ds((s - 2) * SUB, SUB)]

    def rs_second_add(s):
        cols = pl.ds(s * SUB, SUB)
        for c in rs_second(s):
            c.wait_recv()
        other = p2a[:, cols] if s < 2 else p2b[:, pl.ds((s - 2) * SUB, SUB)]
        total = acc[me, :, cols] + other
        hid[:, cols] = (hid[:, cols].astype(F32) + total).astype(BF16)

    order = (0, 2, 1, 3)

    hid[...] = hid_in[...]

    for l in range(LAYERS):
        base = l * CHUNKS
        norm_into(hid, l, x_act, 0)
        for a in range(3):
            weights_relay_last(l, a)
        kv_start(l, 0, 0)
        for a in range(3):
            weights_arrived(l, a)
        tile_start(l, 0, 0, 0)

        @pl.loop(0, HEADS)
        def _(h, l=l):
            slot = lax.rem(h, 2)

            @pl.when(h + 1 < HEADS)
            def _():
                tile_start(l, 0, h + 1, 1 - slot)

            tile_wait(slot)
            q = rope(jnp.dot(x_act[...], w_tile[slot], preferred_element_type=F32))
            q_head[h] = (q * HEAD ** -0.5).astype(BF16).astype(F32)

        tile_start(l, 1, 0, 0)
        tile_start(l, 2, 0, 1)
        for h in range(HEADS):
            q_seq[:, h, :] = q_head[h]
        tile_wait(0)
        kn[...] = rope(jnp.dot(x_act[...], w_tile[0], preferred_element_type=F32)).astype(BF16).astype(F32)
        tile_wait(1)
        vn[...] = jnp.dot(x_act[...], w_tile[1], preferred_element_type=F32).astype(BF16).astype(F32)
        kn_out[l] = kn[...].astype(BF16)
        vn_out[l] = vn[...].astype(BF16)

        weights_relay_last(l, 3)
        if l == 1:
            chunk_start(base + 3)

        @pl.loop(0, GROUPS)
        def _(i, l=l):
            attention_step(l, i)

        if l == 1:
            chunk_start(base + 4)
        for h in range(HEADS):
            a_flat[:, pl.ds(h * HEAD, HEAD)] = a_seq[:, h, :].astype(BF16)
        weights_arrived(l, 3)
        tile_start(l, 3, 0, 0)

        @pl.loop(0, HEADS)
        def _(n, l=l):
            slot = lax.rem(n, 2)

            @pl.when(n + 1 < HEADS)
            def _():
                tile_start(l, 3, n + 1, 1 - slot)

            tile_wait(slot)
            cols = al(n, HEAD)
            part = jnp.dot(a_flat[...], w_tile[slot], preferred_element_type=F32)
            hid[:, cols] = (hid[:, cols].astype(F32) + part).astype(BF16)

        norm_into(hid, LAYERS + l, y_full.at[l], me * ROWS)
        ys = y_sends(l)
        for c in ys.values():
            c.start()
        if l == 1:
            chunk_start(base + 5)
        for m in (2, 4, 6):
            ys[m].wait_recv()
            y_relay(l, m).start()
        ys[1].wait_recv()
        for m in (2, 4, 6):
            y_relay(l, m).wait_recv()

        if l == 0:
            for a in range(4):
                weights_start(1, a)

        def start_next(k, l=l):
            nxt = l * CHUNKS + k + (AHEAD if l == 0 else 6)

            @pl.when(nxt < (CHUNKS if l == 0 else 2 * CHUNKS))
            def _():
                chunk_start(nxt)

        def first_down():
            @pl.loop(0, D // SUB)
            def _(s):
                down_piece(s, True)

        def more_down():
            @pl.loop(0, D // SUB)
            def _(s):
                down_piece(s, False)

        start_next(0)
        mlp_chunk(l, 0, first_down)

        @pl.loop(1, CHUNKS - 1)
        def _(k, l=l):
            start_next(k)
            mlp_chunk(l, k, more_down)

        if l == 0:
            chunk_start(CHUNKS)

        def last_down():
            for s in order:
                down_piece(s, False)
                for c in rs_core(s):
                    c.start()

        mlp_chunk(l, CHUNKS - 1, last_down)
        for s in order:
            rs_core_add(s)
            for c in rs_first(s):
                c.start()
        if l == 0:
            chunk_start(CHUNKS + 1)
        for s in order:
            rs_first_add(s)
            for c in rs_second(s):
                c.start()
        if l == 0:
            chunk_start(CHUNKS + 2)
        for s in order:
            rs_second_add(s)
        for s in order:
            for c in rs_core(s) + rs_first(s) + rs_second(s):
                c.wait_send()

    hid_out[...] = hid[...]

    for c in gain_copies:
        c.wait_send()
    for l in range(LAYERS):
        for a in range(4):
            for c in forwards(l, a):
                c.wait_send()
            for c in relays(l, a):
                c.wait_send()
        for c in y_sends(l).values():
            c.wait_send()
        for m in (2, 4, 6):
            y_relay(l, m).wait_send()

    @pl.loop(0, LAYERS * CHUNKS)
    def _(g):
        chunk_wait(chunk_s, g)


def run_layers(*operands):
    any_spec = pl.BlockSpec(memory_space=pl.ANY)
    vmem = pl.BlockSpec(memory_space=pltpu.VMEM)
    sds = jax.ShapeDtypeStruct
    dma = pltpu.SemaphoreType.DMA
    return pl.pallas_call(
        layers_kernel,
        name="layers",
        out_shape=[
            sds((ROWS, D), BF16), sds((LAYERS, ROWS, HEAD), BF16), sds((LAYERS, ROWS, HEAD), BF16),
            sds((LAYERS, WAYS, SHARD, D), BF16), sds((LAYERS, WAYS, SHARD, HEAD), BF16),
            sds((LAYERS, WAYS, SHARD, HEAD), BF16), sds((LAYERS, WAYS, SHARD, D), BF16),
            sds((LAYERS, CHUNKS, D, CHUNK), BF16), sds((LAYERS, CHUNKS, D, CHUNK), BF16),
        ],
        in_specs=[vmem] * 5 + [any_spec] * 17,
        out_specs=[vmem] * 3 + [any_spec] * 6,
        scratch_shapes=[
            pltpu.VMEM((WAYS, 8, SHARD), F32),
            pltpu.VMEM((ROWS, D), BF16),
            pltpu.VMEM((ROWS, D), BF16),
            pltpu.VMEM((HEADS, ROWS, HEAD), F32),
            pltpu.VMEM((ROWS, HEADS, HEAD), F32),
            pltpu.VMEM((ROWS, HEADS, HEAD), F32),
            pltpu.VMEM((ROWS, D), BF16),
            pltpu.VMEM((ROWS, HEAD), F32),
            pltpu.VMEM((ROWS, HEAD), F32),
            pltpu.VMEM((2, GROUP, SMAX, HEAD), BF16),
            pltpu.VMEM((2, GROUP, SMAX, HEAD), BF16),
            pltpu.VMEM((2, D, HEAD), BF16),
            pltpu.VMEM((LAYERS, BATCH, D), BF16),
            pltpu.VMEM((D, CHUNK), BF16),
            pltpu.VMEM((D, CHUNK), BF16),
            pltpu.VMEM((CHUNK, D), BF16),
            pltpu.VMEM((BATCH, CHUNK), BF16),
            pltpu.VMEM((WAYS, ROWS, D), F32),
            pltpu.VMEM((4, ROWS, D), F32),
            pltpu.VMEM((2, ROWS, D // 2), F32),
            pltpu.VMEM((2, ROWS, D // 2), F32),
            pltpu.VMEM((ROWS, D // 2), F32),
            pltpu.VMEM((ROWS, D // 2), F32),
            dma((WAYS,)), dma((WAYS,)),
            dma((LAYERS, 4, 2)), dma((LAYERS, 4, 2)),
            dma((LAYERS, 4, 4)), dma((LAYERS, 4, 4)),
            dma((LAYERS * CHUNKS, 2)), dma((LAYERS * CHUNKS, 2)),
            dma((LAYERS, WAYS)), dma((LAYERS, WAYS)),
            dma((3, 4, 4)), dma((3, 4, 4)),
            dma((2,)), dma((2, 2)), dma((2,)), dma((1,)),
        ],
        compiler_params=pltpu.CompilerParams(collective_id=0, has_side_effects=True, vmem_limit_bytes=60 * 2**20),
        cost_estimate=pl.CostEstimate(flops=60 * 10**9, bytes_accessed=300 * 10**6, transcendentals=0),
    )(*operands)


def copy_kernel(k_in, v_in, k_out, v_out):
    k_out[...] = k_in[...]
    v_out[...] = v_in[...]


def copy_caches(k_cache, v_cache):
    spec = pl.BlockSpec((1, 16, SMAX, HEAD), lambda l, i: (l, i, 0, 0))
    shape = jax.ShapeDtypeStruct(k_cache.shape, k_cache.dtype)
    return pl.pallas_call(
        copy_kernel, name="copy_caches", grid=(LAYERS, ROWS // 16), in_specs=[spec, spec], out_specs=[spec, spec], out_shape=[shape, shape],
        compiler_params=pltpu.CompilerParams(vmem_limit_bytes=40 * 2**20),
        cost_estimate=pl.CostEstimate(flops=20 * 10**9, bytes_accessed=4 * k_cache.size * 2, transcendentals=0),
    )(k_cache, v_cache)


SLAB = 16


def place_kernel(positions, kn, vn, k_in, v_in, k_out, v_out, k_slab, v_slab, sems):
    def slab(ref, l, s):
        base = pl.multiple_of((positions[s] // SLAB) * SLAB, SLAB)
        return ref.at[l, s, pl.ds(base, SLAB), :]

    for l in range(LAYERS):
        @pl.loop(0, ROWS)
        def _(s, l=l):
            pltpu.make_async_copy(slab(k_out, l, s), k_slab.at[l, s], sems.at[0]).start()
            pltpu.make_async_copy(slab(v_out, l, s), v_slab.at[l, s], sems.at[1]).start()

    pltpu.make_async_copy(k_slab, k_slab, sems.at[0]).wait()
    pltpu.make_async_copy(v_slab, v_slab, sems.at[1]).wait()
    row = lax.broadcasted_iota(jnp.int32, (SLAB, HEAD), 0)
    for l in range(LAYERS):
        @pl.loop(0, ROWS // 8)
        def _(i, l=l):
            k8 = kn[l, al(i, 8), :].astype(F32)
            v8 = vn[l, al(i, 8), :].astype(F32)
            for j in range(8):
                s = i * 8 + j
                hit = row == lax.rem(positions[s], SLAB)
                k_slab[l, s] = jnp.where(hit, k8[j:j + 1], k_slab[l, s].astype(F32)).astype(BF16)
                v_slab[l, s] = jnp.where(hit, v8[j:j + 1], v_slab[l, s].astype(F32)).astype(BF16)

    for l in range(LAYERS):
        @pl.loop(0, ROWS)
        def _(s, l=l):
            pltpu.make_async_copy(k_slab.at[l, s], slab(k_out, l, s), sems.at[2]).start()
            pltpu.make_async_copy(v_slab.at[l, s], slab(v_out, l, s), sems.at[3]).start()

    pltpu.make_async_copy(k_slab, k_slab, sems.at[2]).wait()
    pltpu.make_async_copy(v_slab, v_slab, sems.at[3]).wait()


def place_rows(positions, kn, vn, k_copy, v_copy):
    any_spec = pl.BlockSpec(memory_space=pl.ANY)
    vmem = pl.BlockSpec(memory_space=pltpu.VMEM)
    shape = jax.ShapeDtypeStruct(k_copy.shape, k_copy.dtype)
    return pl.pallas_call(
        place_kernel, name="place_rows",
        in_specs=[pl.BlockSpec(memory_space=pltpu.SMEM), vmem, vmem, any_spec, any_spec],
        out_specs=[any_spec, any_spec], out_shape=[shape, shape], input_output_aliases={3: 0, 4: 1},
        scratch_shapes=[pltpu.VMEM((LAYERS, ROWS, SLAB, HEAD), BF16), pltpu.VMEM((LAYERS, ROWS, SLAB, HEAD), BF16), pltpu.SemaphoreType.DMA((4,))],
        compiler_params=pltpu.CompilerParams(vmem_limit_bytes=40 * 2**20),
    )(positions, kn, vn, k_copy, v_copy)


def solution(mesh):
    batch_spec = P(("dp", "w"))
    cache_spec = P(None, ("dp", "w"))
    gain_spec = P(None, "w")
    weight_spec = P(None, "w", None)
    x_swap = [(s, s ^ 2) for s in range(WAYS)]
    y_swap = [(s, s ^ 4) for s in range(WAYS)]

    def per_device(hidden, positions, k_cache, v_cache, attn_norm, w_query, w_key, w_value, w_out, mlp_norm, w_gate, w_up, w_down):
        attn_weights = (w_query, w_key, w_value, w_out)
        from_x = tuple(lax.ppermute(w, "w", x_swap) for w in attn_weights)
        from_y = tuple(lax.ppermute(w, "w", y_swap) for w in attn_weights)
        k_copy, v_copy = copy_caches(k_cache[:, :, 0], v_cache[:, :, 0])
        cos_tab, sin_tab = rope_tables(positions)
        pos_rep = jnp.repeat(positions, HEADS)[:, None]
        gains = jnp.concatenate([attn_norm, mlp_norm, attn_norm, mlp_norm], axis=0)
        outs = run_layers(hidden, pos_rep, cos_tab, sin_tab, gains, k_copy, v_copy, *attn_weights, *from_x, *from_y, w_gate, w_up, w_down)
        hidden_out, k_new, v_new = outs[:3]
        k_out, v_out = place_rows(positions, k_new, v_new, k_copy, v_copy)
        return hidden_out, k_out[:, :, None], v_out[:, :, None]

    in_specs = (batch_spec, batch_spec, cache_spec, cache_spec, gain_spec, weight_spec, weight_spec, weight_spec, weight_spec, gain_spec, weight_spec, weight_spec, weight_spec)
    out_specs = (batch_spec, cache_spec, cache_spec)
    return jax.shard_map(per_device, mesh=mesh, in_specs=in_specs, out_specs=out_specs, check_vma=False)
```

time: 2140 us -> 680 us (0.32)
  waiting for transfers between devices: 1720 us -> 52.2 us
  Pallas kernels: 0 us -> 607 us
  matrix products: 220 us -> 0 us
  other arithmetic: 94.4 us -> 1.58 us
  blocking collectives: 46.2 us -> 0 us
  local copies, waits for them, and re-layouts: 48.1 us -> 5.07 us
    all_gather x14 -> x0, waiting for transfers between devices: 1710 us -> none  [gather_rows(): return lax.all_gather(row_shard, 'w', axis=0, tiled=True)]
    pallas_call x0 -> x3, Pallas kernels: none -> 607 us  [the longest x1 549 us: run_layers(): pl.pallas_call(layers_kernel, name='layers', out_shape=[sds((ROWS, D), BF...]
    dot_general x16 -> x0, matrix products: 220 us -> none  [the longest x2 92.9 us: per_device(): jnp.dot(mlp_hidden, gather_rows(w_down[layer_idx]), preferred_element_typ...]
    ppermute x0 -> x8, waiting for transfers between devices: none -> 52.2 us  [the longest x4 48.5 us: per_device(): from_x = tuple((lax.ppermute(w, 'w', x_swap) for w in attn_weights))]
    all_gather x4 -> x0, blocking collectives: 46.2 us -> none  [gather_rows(): return lax.all_gather(row_shard, 'w', axis=0, tiled=True)]
    select_n x2 -> x0, other arithmetic: 44.9 us -> none  [the longest x1 33 us: attention_core(): k_layer = jnp.where(write_mask, k_rot[:, :, None, :], k_layer)]
    slice x9 -> x0, local copies, waits for them, and re-layouts: 44.8 us -> none  [the longest x1 12 us: per_device(): w_down[layer_idx]]
    unnamed x2 -> x0, other arithmetic: 23 us -> none
  transfers between devices with their start and end apart: 14 -> 8, of which waited for: 11 -> 3; matrix products, arithmetic and copies ran while one was open for 15% -> 0% of each run, Pallas kernels for 0% -> 7%
where the time goes in v2:
time: 680 us; the launch traced here: 679 us
  Pallas kernels  607 us (89%)
  waiting for transfers between devices  52.2 us (8%)
  starting transfers between devices  12.7 us (2%)
    pallas_call x1, Pallas kernels, run_layers(): pl.pallas_call(layers_kernel, name='layers', out_shape=[sds((ROWS, D), BF...  549 us
    ppermute x4, waiting for transfers between devices, per_device(): from_x = tuple((lax.ppermute(w, 'w', x_swap) for w in attn_weights))  48.5 us
    pallas_call x1, Pallas kernels, copy_caches(): pl.pallas_call(copy_kernel, name='copy_caches', grid=(LAYERS, ROWS // 16)...  45 us
  transfers between devices with their start and end apart: 8, of which 3 were waited for; matrix products, arithmetic and copies ran while one was open for 0% of the time, Pallas kernels for 7%

profile of v2, /device:TPU:0, one launch (start us, length us, event | category | flops | bytes accessed | tf_op | source)
XLA Modules:
  0.0 678.8 jit_solution(16289814861167956300)
XLA Ops:
  0.6 3.4 collective-permute-start.1
  4.0 1.5 collective-permute-start.5
  5.5 0.5 collective-permute-start
  6.0 0.0 collective-permute-start.4
  6.1 2.0 collective-permute-start.3
  8.0 3.1 collective-permute-done.1.kx
  11.2 0.0 copy-start.8
  11.2 2.0 collective-permute-start.7
  13.2 0.0 collective-permute-done.5.ky
  13.2 0.0 copy-start.9
  13.2 1.5 collective-permute-start.2
  14.7 0.0 copy-start.4
  14.7 0.0 copy-start.5
  14.7 0.0 copy-start.7
  14.7 0.0 copy-start.2
  14.7 45.0 %copy_caches.1 = (bf16[2,128,256,256]{3,2,1,0:T(8,128)(2,1)}, bf16[2,128,256,256]{3,2,1,0:T(8,128)(2,1)}) custom-call(bf16[2,128,256,256]{3,2,1,0:T(8,128)(2,1)} %bitcast.10, bf16[2,128,256,256]{3,2,1,0:T(8,128)(2,1)} %bitcast.11), custom_call_target="tpu_custom_call" | custom-call | flops 20000000000 | bytes 134217728 | tf_op jit(solution)/shard_map/copy_caches/pallas_call | solution.py:507
  59.8 0.0 copy-done.8
  59.8 0.0 copy-done.9
  59.8 0.0 copy-done.4
  59.8 0.0 copy-done.5
  59.8 0.6 pad_maximum_fusion.gains_own
  60.4 45.4 %collective-permute-done.2.vx = bf16[2,256,256]{2,1,0:T(8,128)(2,1)S(1)} collective-permute-done((bf16[2,256,256]{2,1,0:T(8,128)(2,1)}, bf16[2,256,256]{2,1,0:T(8,128)(2,1)S(1)}, u32[]{:S(2)}, u32[]{:S(2)}) %collective-permute-start.2) | collective-permute-done | bytes 262176 | tf_op jit(solution)/shard_map/ppermute | solution.py:575
  105.8 0.0 copy-done.7
  105.8 0.0 copy-start.10
  105.8 1.8 collective-permute-start.6
  107.6 0.0 copy-done.2
  107.6 0.1 broadcast_in_dim.11
  107.7 1.0 broadcast_in_dim_reshape.4.pos_rep
  108.7 1.0 multiply_sine_fusion
  109.6 3.7 collective-permute-done.6.vy
  113.3 0.0 copy-start.11
  113.3 0.0 collective-permute-done.qx
  113.3 0.0 copy-start.6
  113.3 0.0 collective-permute-done.4.qy
  113.3 0.0 collective-permute-done.3.ox
  113.3 0.0 collective-permute-done.7.oy
  113.3 0.0 copy-done.10
  113.3 0.6 copy-done.11
  114.0 0.7 copy-done.6
  114.7 549.0 %layers.1 = (bf16[128,2048]{1,0:T(8,128)(2,1)}, bf16[2,128,256]{2,1,0:T(8,128)(2,1)}, bf16[2,128,256]{2,1,0:T(8,128)(2,1)}, bf16[2,8,256,2048]{3,2,1,0:T(8,128)(...) custom-call(bf16[128,2048]{1,0:T(8,128)(2,1)} %hid_in.1, ...), custom_call_target="tpu_custom_call" | custom-call | flops 60000002048 | bytes 300000000 | tf_op jit(solution)/shard_map/layers/pallas_call | solution.py:451
  663.7 0.0 copy-start
  663.7 0.9 copy-done
  664.6 0.0 copy-start.1
  664.6 0.9 copy-done.1
  665.5 0.0 copy-start.3
  665.5 12.5 %place_rows.1 = (bf16[2,128,256,256]{3,2,1,0:T(8,128)(2,1)}, bf16[2,128,256,256]{3,2,1,0:T(8,128)(2,1)}) custom-call(s32[128]{0:T(128)S(1)} %copy-done.2, bf16[2,128,256]{2,1,0:T(8,128)(2,1)S(1)} %copy-done, bf16[2,128,256]{2,1,0:T(8,128)(2,1)S(1)} %copy-done.1, ...), custom_call_target="tpu_custom_call", output_to_operand_aliasing={{0}: (3, {}), {1}: (4, {})} | custom-call | tf_op jit(solution)/shard_map/place_rows/pallas_call | solution.py:556
  678.0 0.0 copy-done.3
  678.0 0.8 copy.26
  (2 shorter events, 0.0 us)
Async XLA Ops:
  0.6 10.5 %collective-permute-start.1 = (bf16[2,256,256]{2,1,0:T(8,128)(2,1)}, bf16[2,256,256]{2,1,0:T(8,128)(2,1)S(1)}, u32[]{:S(2)}, u32[]{:S(2)}) collective-permute-start(bf16[2,256,256]{2,1,0:T(8,128)(2,1)} %wk.1), channel_id=1, source_target_pairs={{0,2},{1,3},{2,0},{3,1},{4,6},{5,7},{6,4},{7,5}} | collective-permute-start | bytes 786440 | tf_op jit(solution)/shard_map/ppermute | solution.py:575
  4.0 9.2 %collective-permute-start.5 = (bf16[2,256,256]{2,1,0:T(8,128)(2,1)}, bf16[2,256,256]{2,1,0:T(8,128)(2,1)S(1)}, u32[]{:S(2)}, u32[]{:S(2)}) collective-permute-start(bf16[2,256,256]{2,1,0:T(8,128)(2,1)} %wk.1), channel_id=1, source_target_pairs={{0,4},{1,5},{2,6},{3,7},{4,0},{5,1},{6,2},{7,3}} | collective-permute-start | bytes 786440 | tf_op jit(solution)/shard_map/ppermute | solution.py:576
  5.5 107.8 %collective-permute-start = (bf16[2,256,2048]{2,1,0:T(8,128)(2,1)}, bf16[2,256,2048]{2,1,0:T(8,128)(2,1)S(1)}, u32[]{:S(2)}, u32[]{:S(2)}) collective-permute-start(bf16[2,256,2048]{2,1,0:T(8,128)(2,1)} %wq.1), channel_id=1, source_target_pairs={{0,2},{1,3},{2,0},{3,1},{4,6},{5,7},{6,4},{7,5}} | collective-permute-start | bytes 6291464 | tf_op jit(solution)/shard_map/ppermute | solution.py:575
  6.0 107.2 %collective-permute-start.4 = (bf16[2,256,2048]{2,1,0:T(8,128)(2,1)}, bf16[2,256,2048]{2,1,0:T(8,128)(2,1)}, u32[]{:S(2)}, u32[]{:S(2)}) collective-permute-start(bf16[2,256,2048]{2,1,0:T(8,128)(2,1)} %wq.1), channel_id=1, source_target_pairs={{0,4},{1,5},{2,6},{3,7},{4,0},{5,1},{6,2},{7,3}} | collective-permute-start | bytes 6291464 | tf_op jit(solution)/shard_map/ppermute | solution.py:576
  6.1 107.2 %collective-permute-start.3 = (bf16[2,256,2048]{2,1,0:T(8,128)(2,1)}, bf16[2,256,2048]{2,1,0:T(8,128)(2,1)}, u32[]{:S(2)}, u32[]{:S(2)}) collective-permute-start(bf16[2,256,2048]{2,1,0:T(8,128)(2,1)} %wo.1), channel_id=1, source_target_pairs={{0,2},{1,3},{2,0},{3,1},{4,6},{5,7},{6,4},{7,5}} | collective-permute-start | bytes 6291464 | tf_op jit(solution)/shard_map/ppermute | solution.py:575
  11.2 48.6 %copy-start.8 = (bf16[2,256,256]{2,1,0:T(8,128)(2,1)}, bf16[2,256,256]{2,1,0:T(8,128)(2,1)S(1)}, u32[]{:S(2)}) copy-start(bf16[2,256,256]{2,1,0:T(8,128)(2,1)S(1)} %collective-permute-done.1.kx) | copy-start | bytes 786436
  11.2 102.1 %collective-permute-start.7 = (bf16[2,256,2048]{2,1,0:T(8,128)(2,1)}, bf16[2,256,2048]{2,1,0:T(8,128)(2,1)}, u32[]{:S(2)}, u32[]{:S(2)}) collective-permute-start(bf16[2,256,2048]{2,1,0:T(8,128)(2,1)} %wo.1), channel_id=1, source_target_pairs={{0,4},{1,5},{2,6},{3,7},{4,0},{5,1},{6,2},{7,3}} | collective-permute-start | bytes 6291464 | tf_op jit(solution)/shard_map/ppermute | solution.py:576
  13.2 46.5 %copy-start.9 = (bf16[2,256,256]{2,1,0:T(8,128)(2,1)}, bf16[2,256,256]{2,1,0:T(8,128)(2,1)S(1)}, u32[]{:S(2)}) copy-start(bf16[2,256,256]{2,1,0:T(8,128)(2,1)S(1)} %collective-permute-done.5.ky) | copy-start | bytes 786436
  13.2 92.6 %collective-permute-start.2 = (bf16[2,256,256]{2,1,0:T(8,128)(2,1)}, bf16[2,256,256]{2,1,0:T(8,128)(2,1)S(1)}, u32[]{:S(2)}, u32[]{:S(2)}) collective-permute-start(bf16[2,256,256]{2,1,0:T(8,128)(2,1)} %wv.1), channel_id=1, source_target_pairs={{0,2},{1,3},{2,0},{3,1},{4,6},{5,7},{6,4},{7,5}} | collective-permute-start | bytes 786440 | tf_op jit(solution)/shard_map/ppermute | solution.py:575
  14.7 45.1 %copy-start.4 = (f32[2,256]{1,0:T(2,128)S(1)}, f32[2,256]{1,0:T(2,128)}, u32[]{:S(2)}) copy-start(f32[2,256]{1,0:T(2,128)} %param.22) | copy-start | bytes 6148
  14.7 45.1 %copy-start.5 = (f32[2,256]{1,0:T(2,128)S(1)}, f32[2,256]{1,0:T(2,128)}, u32[]{:S(2)}) copy-start(f32[2,256]{1,0:T(2,128)} %param.17) | copy-start | bytes 6148
  14.7 91.1 %copy-start.7 = (bf16[2,256,256]{2,1,0:T(8,128)(2,1)S(1)}, bf16[2,256,256]{2,1,0:T(8,128)(2,1)}, u32[]{:S(2)}) copy-start(bf16[2,256,256]{2,1,0:T(8,128)(2,1)} %wv.1) | copy-start | bytes 786436
  14.7 92.9 %copy-start.2 = (s32[128]{0:T(128)S(1)}, s32[128]{0:T(128)}, u32[]{:S(2)}) copy-start(s32[128]{0:T(128)} %positions.1) | copy-start | bytes 1540
  105.8 7.5 %copy-start.10 = (bf16[2,256,256]{2,1,0:T(8,128)(2,1)}, bf16[2,256,256]{2,1,0:T(8,128)(2,1)S(1)}, u32[]{:S(2)}) copy-start(bf16[2,256,256]{2,1,0:T(8,128)(2,1)S(1)} %collective-permute-done.2.vx) | copy-start | bytes 786436
  105.8 7.5 %collective-permute-start.6 = (bf16[2,256,256]{2,1,0:T(8,128)(2,1)S(1)}, bf16[2,256,256]{2,1,0:T(8,128)(2,1)S(1)}, u32[]{:S(2)}, u32[]{:S(2)}) collective-permute-start(bf16[2,256,256]{2,1,0:T(8,128)(2,1)S(1)} %copy-done.7), channel_id=1, source_target_pairs={{0,4},{1,5},{2,6},{3,7},{4,0},{5,1},{6,2},{7,3}} | collective-permute-start | bytes 786440 | tf_op jit(solution)/shard_map/ppermute | solution.py:576
  113.3 0.7 copy-start.11
  113.3 1.4 copy-start.6
  663.7 0.9 copy-start
  664.6 0.9 copy-start.1
  665.5 12.5 %copy-start.3 = (bf16[128,2048]{1,0:T(8,128)(2,1)S(1)}, bf16[128,2048]{1,0:T(8,128)(2,1)}, u32[]{:S(2)}) copy-start(bf16[128,2048]{1,0:T(8,128)(2,1)} %get-tuple-element.28) | copy-start | bytes 1572868
